TPU v7x, 256 devices: a whole 4x4x8 slice. The times are simulated.
256 devices in a mesh: gz: 16 (over x, y), gy: 16 (over z, core).
Axes of the slice: x: 4, y: 4, z: 8, core: 2. Of those that a mesh axis runs over, the one named last changes fastest.
Arguments:
- fixed: float32 [512, 1024, 256], P('gz', 'gy'), may hold values from -6 to 6
- moving: float32 [512, 1024, 256], P('gz', 'gy'), may hold values from -6 to 6
Outputs:
- update: float32 [3, 64, 128, 32], P(None, 'gz', 'gy')
- residual: float32 [3, 64, 128, 32], P(None, 'gz', 'gy')
All inputs are finite; a program needn't handle non-finite values.
Results may differ from a plain program's by a relative error of at most 0.0031.
Values sent between devices are 32-bit elements; how exact they have to be, the bound alone decides.
A program may use at most 64 MiB of HBM per device.

v0:
```python
import functools

import jax
import jax.numpy as jnp
from jax import lax
from jax.sharding import Mesh
from jax.sharding import PartitionSpec as P

SPACING = 8
ITERS = 2
GZ = ("gz_0", "gz_1")
GY = ("gy_0", "gy_1")
GZ_GY = ("gz_0", "gz_1", "gy_0", "gy_1")


damping_weight = 8.0


def from_behind(value, axis, steps):
    count = lax.axis_size(axis)
    initial, last = (max(0, -steps), min(count, count - steps))
    return lax.ppermute(value, axis, [(source, source + steps) for source in range(initial, last)])


def by_axis(x, axes):
    return functools.reduce(lax.psum, axes, x)


def with_halo(x, sides, width):
    edges = {}
    for axis, dim in sides:
        size, length = (lax.axis_size(axis), x.shape[dim])
        up = [(i, (i + 1) % size) for i in range(size - 1)]
        last = lax.slice_in_dim(x, length - width, length, axis=dim)
        initial = lax.slice_in_dim(x, 0, width, axis=dim)
        edges[dim] = (
            lax.ppermute(last, axis, up),
            lax.ppermute(initial, axis, [(b, a) for a, b in up]),
        )
    done = []
    for _, dim in sides:
        low, high = edges[dim]
        around = [(width, width) if d in done else (0, 0) for d in range(x.ndim)]
        x = jnp.concatenate([jnp.pad(low, around), x, jnp.pad(high, around)], axis=dim)
        done.append(dim)
    return x


def padded_2(cells, sides, width):
    for axis, dim in sides:
        count = lax.axis_size(axis)
        ends = count - 1
        head = lax.slice_in_dim(cells, 0, width, axis=dim)
        tail = lax.slice_in_dim(cells, cells.shape[dim] - width, cells.shape[dim], axis=dim)
        cells = jnp.concatenate(
            [
                lax.ppermute(tail, axis, [(i, (i + 1) % count) for i in range(ends)]),
                cells,
                lax.ppermute(head, axis, [((i + 1) % count, i) for i in range(ends)]),
            ],
            axis=dim,
        )
    return cells


def basis_matrix(count, columns, offset):
    voxel = jnp.arange(count, dtype=jnp.int32)
    cell = voxel // SPACING
    frac = ((voxel % SPACING).astype(jnp.float32) + 0.5) / SPACING
    other = 1.0 - frac
    weights = (
        other**3 / 6.0,
        (3.0 * frac**3 - 6.0 * frac**2 + 4.0) / 6.0,
        (-3.0 * frac**3 + 3.0 * frac**2 + 3.0 * frac + 1.0) / 6.0,
        frac**3 / 6.0,
    )
    index = jnp.arange(columns, dtype=jnp.int32)
    matrix = jnp.zeros((count, columns), jnp.float32)
    for tap in range(4):
        match = index[None, :] == (cell - 1 + tap + offset)[:, None]
        matrix = matrix + jnp.where(match, weights[tap][:, None], jnp.float32(0.0))
    return matrix


def decode(control, along_z, along_y, along_x):
    hp = lax.Precision.HIGHEST
    inner = jnp.einsum("cabe,xe->cabx", control, along_x, precision=hp)
    inner = jnp.einsum("yb,cabx->cayx", along_y, inner, precision=hp)
    return jnp.einsum("za,cayx->czyx", along_z, inner, precision=hp)


def encode(volume, along_z, along_y, along_x):
    hp = lax.Precision.HIGHEST
    inner = jnp.einsum("za,czyx->cayx", along_z, volume, precision=hp)
    inner = jnp.einsum("yb,cayx->cabx", along_y, inner, precision=hp)
    return jnp.einsum("xe,cabx->cabe", along_x, inner, precision=hp)


def derivative(padded, axis):
    length = padded.shape[axis] - 6

    def part(shift_by):
        return lax.slice_in_dim(padded, 3 + shift_by, 3 + shift_by + length, axis=axis)

    return (45.0 * (part(1) - part(-1)) - 9.0 * (part(2) - part(-2)) + (part(3) - part(-3))) / 60.0


def fold_rims(extended):
    depth = extended.shape[1] - 4
    from_above = from_behind(extended[:, 0:2], GZ, -1)
    from_below = from_behind(extended[:, depth + 2 : depth + 4], GZ, 1)
    core = extended[:, 2 : depth + 2]
    core = core.at[:, depth - 2 :].add(from_above).at[:, :2].add(from_below)
    width = core.shape[2] - 4
    from_right = from_behind(core[:, :, 0:2], GY, -1)
    from_left = from_behind(core[:, :, width + 2 : width + 4], GY, 1)
    inner = core[:, :, 2 : width + 2]
    return inner.at[:, :, width - 2 :].add(from_right).at[:, :, :2].add(from_left)


def two_products(residual, image):
    return (by_axis(jnp.sum(residual * residual), GZ_GY), by_axis(jnp.sum(residual * image), GZ_GY))


def shards(fixed, moving):
    slab_z, slab_y, extent = fixed.shape
    mean = 0.5 * (fixed + moving)
    framed = with_halo(mean, ((GZ, 0), (GY, 1)), 3)
    framed = jnp.pad(framed, ((0, 0), (0, 0), (3, 3)))
    gradient = jnp.stack(
        [
            derivative(framed[:, 3:-3, 3:-3], 0),
            derivative(framed[3:-3, :, 3:-3], 1),
            derivative(framed[3:-3, 3:-3, :], 2),
        ]
    ).astype(jnp.bfloat16)
    mismatch = moving - fixed
    ctrl_z = slab_z // SPACING
    ctrl_y = slab_y // SPACING
    ctrl_x = extent // SPACING
    along_z = basis_matrix(slab_z, ctrl_z + 4, 2)
    along_y = basis_matrix(slab_y, ctrl_y + 4, 2)
    along_x = basis_matrix(extent, ctrl_x, 0)
    slopes = gradient.astype(jnp.float32)

    def operate(control):
        extended = padded_2(control, ((GZ, 1), (GY, 2)), 2)
        field = decode(extended, along_z, along_y, along_x)
        volume = slopes * jnp.sum(slopes * field, axis=0)[None]
        return fold_rims(encode(volume, along_z, along_y, along_x)) + damping_weight * control

    rhs = -fold_rims(encode(slopes * mismatch[None], along_z, along_y, along_x))
    update = jnp.zeros_like(rhs)
    residual = rhs
    image = operate(residual)
    norm_now, product = two_products(residual, image)
    alpha = norm_now / product
    direction, along = (residual, image)
    for step_index in range(ITERS):
        update = update + alpha * direction
        residual = residual - alpha * along
        if step_index + 1 < ITERS:
            image = operate(residual)
            norm_next, product = two_products(residual, image)
            ratio = norm_next / norm_now
            alpha = norm_next / (product - ratio * norm_next / alpha)
            direction = residual + ratio * direction
            along = image + ratio * along
            norm_now = norm_next
    return (update, residual)


def solution(mesh):
    finer = Mesh(mesh.devices.reshape(4, 4, 8, 2), ("gz_0", "gz_1", "gy_0", "gy_1"))
    placed = (P(GZ, GY, None), P(GZ, GY, None))
    return jax.shard_map(
        shards,
        mesh=finer,
        in_specs=placed,
        out_specs=(P(None, GZ, GY, None), P(None, GZ, GY, None)),
        check_vma=False,
    )
```

profile of v0, /device:TPU:1, one launch (start us, length us, event | category | flops | bytes accessed | tf_op | source)
XLA Modules:
  0.0 259.5 jit_solution(3940282998905295446)
XLA Ops:
  0.6 4.8 %fusion.34 = f32[32,64,256]{2,0,1:T(8,128)S(1)} fusion(f32[32,64,256]{2,1,0:T(8,128)} %param.27, f32[32,64,256]{2,1,0:T(8,128)} %param.26), kind=kLoop, calls=%fused_computation.65 | loop fusion | flops 1048576 | bytes 6291456 | tf_op jit(solution)/shard_map/mul | solution.py:127
  6.9 4.7 %collective-permute-start.1 = (f32[3,64,256]{2,0,1:T(4,128)S(1)}, f32[3,64,256]{2,0,1:T(4,128)S(1)}, u32[]{:S(2)}, u32[]{:S(2)}) collective-permute-start(f32[3,64,256]{2,0,1:T(4,128)S(1)} %get-tuple-element.168), channel_id=1, source_target_pairs={{0,16},{16,32},{32,48},{48,64},{64,80},{80,96},{96,112},{112,128},... | collective-permute-start | bytes 589832 | tf_op jit(solution)/shard_map/ppermute | solution.py:37
  11.5 5.0 %collective-permute-start.2 = (f32[32,3,256]{2,0,1:T(8,128)S(1)}, f32[32,3,256]{2,0,1:T(8,128)S(1)}, u32[]{:S(2)}, u32[]{:S(2)}) collective-permute-start(f32[32,3,256]{2,0,1:T(8,128)S(1)} %get-tuple-element.171), channel_id=1, source_target_pairs={{1,0},{2,1},{3,2},{4,3},{5,4},{6,5},{7,6},{8,7},{9,8},{10,9},{11,1... | collective-permute-start | bytes 294920 | tf_op jit(solution)/shard_map/ppermute | solution.py:38
  25.4 5.1 %fusion.55 = (bf16[1,32,64,256]{3,1,2,0:T(8,128)(2,1)S(1)}, bf16[1,32,64,256]{3,1,2,0:T(8,128)(2,1)S(1)}) fusion(f32[38,67,256]{2,0,1:T(8,128)S(1)} %get-tuple-element.167, f32[38,67,256]{2,0,1:T(8,128)S(1)} %get-tuple-element.166, f32[38,70,262]{2,0,1:T(8,128)S(1)} %select_maximum_fusion), kind=kLoop, calls=%fused_computation.82 | loop fusion | flops 9437184 | bytes 27262976 | tf_op jit(solution)/shard_map/stack | solution.py:130
  33.8 4.0 %fusion.45 = f32[3,8,64,256]{3,1,2,0:T(8,128)S(1)} fusion(f32[32,64,256]{2,0,1:T(8,128)S(1)} %copy.6, f32[32]{0:T(128)S(1)} %get-tuple-element.209, s32[32]{0:T(128)S(1)} %get-tuple-element.214, f32[32]{0:T(128)S(1)} %get-tuple-element.201, s32[32]{0:T(128)S(1)} %get-tuple-element.216, f32[32]{0:T(128)S(1)} %get-tuple-element.208, ...), kind=kOutput, calls=%fused_computation.76 | convolution fusion | flops 157289216 | bytes 6816768 | tf_op jit(solution)/shard_map/za,czyx->cayx/dot_general | solution.py:94
  41.0 4.0 %collective-permute-start.5 = (f32[3,2,12,32]{3,2,1,0:T(8,128)S(1)}, f32[3,2,12,32]{3,2,1,0:T(8,128)S(1)}, u32[]{:S(2)}, u32[]{:S(2)}) collective-permute-start(f32[3,2,12,32]{3,2,1,0:T(8,128)S(1)} %get-tuple-element.176), channel_id=1, source_target_pairs={{0,16},{16,32},{32,48},{48,64},{64,80},{80,96},{96,112},{112,128},... | collective-permute-start | bytes 27656 | tf_op jit(solution)/shard_map/ppermute | solution.py:22
  49.8 3.8 %collective-permute-start.7 = (f32[3,4,2,32]{3,2,1,0:T(2,128)S(1)}, f32[3,4,2,32]{3,2,1,0:T(2,128)S(1)}, u32[]{:S(2)}, u32[]{:S(2)}) collective-permute-start(f32[3,4,2,32]{3,2,1,0:T(2,128)S(1)} %get-tuple-element.188), channel_id=1, source_target_pairs={{0,1},{1,2},{2,3},{3,4},{4,5},{5,6},{6,7},{7,8},{8,9},{9,10},{10,1... | collective-permute-start | bytes 9224 | tf_op jit(solution)/shard_map/ppermute | solution.py:22
  54.3 4.0 %collective-permute-start.8 = (f32[3,2,8,32]{3,2,1,0:T(8,128)S(1)}, f32[3,2,8,32]{3,2,1,0:T(8,128)S(1)}, u32[]{:S(2)}, u32[]{:S(2)}) collective-permute-start(f32[3,2,8,32]{3,2,1,0:T(8,128)S(1)} %get-tuple-element.192), channel_id=1, source_target_pairs={{0,16},{16,32},{32,48},{48,64},{64,80},{80,96},{96,112},{112,128},... | collective-permute-start | bytes 18440 | tf_op jit(solution)/shard_map/ppermute | solution.py:57
  63.1 5.4 %collective-permute-start.10 = (f32[3,8,2,32]{3,2,1,0:T(2,128)S(1)}, f32[3,8,2,32]{3,2,1,0:T(2,128)S(1)}, u32[]{:S(2)}, u32[]{:S(2)}) collective-permute-start(f32[3,8,2,32]{3,2,1,0:T(2,128)S(1)} %get-tuple-element.186), channel_id=1, source_target_pairs={{0,1},{1,2},{2,3},{3,4},{4,5},{5,6},{6,7},{7,8},{8,9},{9,10},{10,1... | collective-permute-start | bytes 18440 | tf_op jit(solution)/shard_map/ppermute | solution.py:57
  75.5 6.2 %fusion.1 = f32[32,64,256]{2,0,1:T(8,128)S(1)} fusion(f32[3,8,64,256]{3,2,1,0:T(8,128)S(1)} %convolution_bitcast_fusion.1, f32[32]{0:T(128)S(1)} %get-tuple-element.209, s32[32]{0:T(128)S(1)} %get-tuple-element.214, f32[32]{0:T(128)S(1)} %get-tuple-element.201, s32[32]{0:T(128)S(1)} %get-tuple-element.216, f32[32]{0:T(128)S(1)} %get-tuple-element.208, ...), kind=kOutput, calls=%fused_computation.8 | convolution fusion | flops 158337792 | bytes 6816768 | tf_op jit(solution)/shard_map/za,cayx->czyx/dot_general | solution.py:89
  81.7 4.1 %fusion.44 = f32[3,8,64,256]{3,1,2,0:T(8,128)S(1)} fusion(f32[32,64,256]{2,0,1:T(8,128)S(1)} %fusion.1, f32[32]{0:T(128)S(1)} %get-tuple-element.209, s32[32]{0:T(128)S(1)} %get-tuple-element.214, f32[32]{0:T(128)S(1)} %get-tuple-element.201, s32[32]{0:T(128)S(1)} %get-tuple-element.216, f32[32]{0:T(128)S(1)} %get-tuple-element.208, ...), kind=kOutput, calls=%fused_computation.75 | convolution fusion | flops 157289216 | bytes 6816768 | tf_op jit(solution)/shard_map/za,czyx->cayx/dot_general | solution.py:94
  89.0 6.4 %collective-permute-start.13 = (f32[3,2,12,32]{3,2,1,0:T(8,128)S(1)}, f32[3,2,12,32]{3,2,1,0:T(8,128)S(1)}, u32[]{:S(2)}, u32[]{:S(2)}) collective-permute-start(f32[3,2,12,32]{3,2,1,0:T(8,128)S(1)} %get-tuple-element.174), channel_id=1, source_target_pairs={{0,16},{16,32},{32,48},{48,64},{64,80},{80,96},{96,112},{112,128},... | collective-permute-start | bytes 27656 | tf_op jit(solution)/shard_map/ppermute | solution.py:22
  103.6 20.4 %all-reduce.8 = (f32[]{:T(128)}, f32[]{:T(128)}) all-reduce(f32[]{:T(128)} %get-tuple-element.149, f32[]{:T(128)} %get-tuple-element.148), channel_id=1, replica_groups=mesh['gz_0'=4,'gz_1'=4,'gy_0'=8,'gy_1'=2] {'gz_0'}, use_global_device_ids=true, to_apply=%region_1.2 | all-reduce | flops 2 | bytes 16 | tf_op jit(solution)/shard_map/psum | solution.py:26
  123.9 6.6 %all-reduce.6 = (f32[]{:T(128)}, f32[]{:T(128)}) all-reduce(f32[]{:T(128)} %get-tuple-element.160, f32[]{:T(128)} %get-tuple-element.161), channel_id=1, replica_groups=mesh['gz_0'=4,'gz_1'=4,'gy_0'=8,'gy_1'=2] {'gz_1'}, use_global_device_ids=true, to_apply=%region_2.3 | all-reduce | flops 2 | bytes 16 | tf_op jit(solution)/shard_map/psum | solution.py:26
  130.5 19.9 %all-reduce.4 = (f32[]{:T(128)}, f32[]{:T(128)}) all-reduce(f32[]{:T(128)} %get-tuple-element.156, f32[]{:T(128)} %get-tuple-element.157), channel_id=1, replica_groups=mesh['gz_0'=4,'gz_1'=4,'gy_0'=8,'gy_1'=2] {'gy_0'}, use_global_device_ids=true, to_apply=%region_3.4 | all-reduce | flops 2 | bytes 16 | tf_op jit(solution)/shard_map/psum | solution.py:26
  150.4 10.6 %all-reduce.10 = (f32[]{:T(128)}, f32[]{:T(128)}) all-reduce(f32[]{:T(128)} %get-tuple-element.152, f32[]{:T(128)} %get-tuple-element.153), channel_id=1, replica_groups=mesh['gz_0'=4,'gz_1'=4,'gy_0'=8,'gy_1'=2] {'gy_1'}, use_global_device_ids=true, to_apply=%region_4.5 | all-reduce | flops 2 | bytes 16 | tf_op jit(solution)/shard_map/psum | solution.py:26
  170.6 5.3 %collective-permute-start.18 = (f32[3,8,2,32]{3,2,1,0:T(2,128)S(1)}, f32[3,8,2,32]{3,2,1,0:T(2,128)S(1)}, u32[]{:S(2)}, u32[]{:S(2)}) collective-permute-start(f32[3,8,2,32]{3,2,1,0:T(2,128)S(1)} %get-tuple-element.182), channel_id=1, source_target_pairs={{0,1},{1,2},{2,3},{3,4},{4,5},{5,6},{6,7},{7,8},{8,9},{9,10},{10,1... | collective-permute-start | bytes 18440 | tf_op jit(solution)/shard_map/ppermute | solution.py:57
  183.0 6.2 %fusion.3 = f32[32,64,256]{2,0,1:T(8,128)S(1)} fusion(f32[3,8,64,256]{3,2,1,0:T(8,128)S(1)} %convolution_bitcast_fusion, f32[32]{0:T(128)S(1)} %get-tuple-element.209, s32[32]{0:T(128)S(1)} %get-tuple-element.214, f32[32]{0:T(128)S(1)} %get-tuple-element.201, s32[32]{0:T(128)S(1)} %get-tuple-element.216, f32[32]{0:T(128)S(1)} %get-tuple-element.208, ...), kind=kOutput, calls=%fused_computation.10 | convolution fusion | flops 158337792 | bytes 6816768 | tf_op jit(solution)/shard_map/za,cayx->czyx/dot_general | solution.py:89
  189.2 4.1 %fusion.43 = f32[3,8,64,256]{3,1,2,0:T(8,128)S(1)} fusion(f32[32,64,256]{2,0,1:T(8,128)S(1)} %fusion.3, f32[32]{0:T(128)S(1)} %get-tuple-element.209, s32[32]{0:T(128)S(1)} %get-tuple-element.214, f32[32]{0:T(128)S(1)} %get-tuple-element.201, s32[32]{0:T(128)S(1)} %get-tuple-element.216, f32[32]{0:T(128)S(1)} %get-tuple-element.208, ...), kind=kOutput, calls=%fused_computation.74 | convolution fusion | flops 157289216 | bytes 6816768 | tf_op jit(solution)/shard_map/za,czyx->cayx/dot_general | solution.py:94
  196.4 4.0 %collective-permute-start.21 = (f32[3,2,12,32]{3,2,1,0:T(8,128)S(1)}, f32[3,2,12,32]{3,2,1,0:T(8,128)S(1)}, u32[]{:S(2)}, u32[]{:S(2)}) collective-permute-start(f32[3,2,12,32]{3,2,1,0:T(8,128)S(1)} %get-tuple-element.172), channel_id=1, source_target_pairs={{0,16},{16,32},{32,48},{48,64},{64,80},{80,96},{96,112},{112,128},... | collective-permute-start | bytes 27656 | tf_op jit(solution)/shard_map/ppermute | solution.py:22
  208.7 12.5 %all-reduce.7 = (f32[]{:T(128)}, f32[]{:T(128)}) all-reduce(f32[]{:T(128)} %get-tuple-element.147, f32[]{:T(128)} %get-tuple-element.146), channel_id=1, replica_groups=mesh['gz_0'=4,'gz_1'=4,'gy_0'=8,'gy_1'=2] {'gz_0'}, use_global_device_ids=true, to_apply=%region_12.13 | all-reduce | flops 2 | bytes 16 | tf_op jit(solution)/shard_map/psum | solution.py:26
  221.3 6.7 %all-reduce.5 = (f32[]{:T(128)}, f32[]{:T(128)}) all-reduce(f32[]{:T(128)} %get-tuple-element.158, f32[]{:T(128)} %get-tuple-element.159), channel_id=1, replica_groups=mesh['gz_0'=4,'gz_1'=4,'gy_0'=8,'gy_1'=2] {'gz_1'}, use_global_device_ids=true, to_apply=%region_13.14 | all-reduce | flops 2 | bytes 16 | tf_op jit(solution)/shard_map/psum | solution.py:26
  228.0 14.8 %all-reduce.3 = (f32[]{:T(128)}, f32[]{:T(128)}) all-reduce(f32[]{:T(128)} %get-tuple-element.154, f32[]{:T(128)} %get-tuple-element.155), channel_id=1, replica_groups=mesh['gz_0'=4,'gz_1'=4,'gy_0'=8,'gy_1'=2] {'gy_0'}, use_global_device_ids=true, to_apply=%region_14.15 | all-reduce | flops 2 | bytes 16 | tf_op jit(solution)/shard_map/psum | solution.py:26
  242.7 11.0 %all-reduce.9 = (f32[]{:T(128)}, f32[]{:T(128)}) all-reduce(f32[]{:T(128)} %get-tuple-element.150, f32[]{:T(128)} %get-tuple-element.151), channel_id=1, replica_groups=mesh['gz_0'=4,'gz_1'=4,'gy_0'=8,'gy_1'=2] {'gy_1'}, use_global_device_ids=true, to_apply=%region_15.16 | all-reduce | flops 2 | bytes 16 | tf_op jit(solution)/shard_map/psum | solution.py:26
  (111 shorter events, 72.3 us)
Async XLA Ops:
  5.6 14.8 %collective-permute-start = (f32[3,64,256]{2,0,1:T(4,128)S(1)}, f32[3,64,256]{2,0,1:T(4,128)S(1)}, u32[]{:S(2)}, u32[]{:S(2)}) collective-permute-start(f32[3,64,256]{2,0,1:T(4,128)S(1)} %get-tuple-element.169), channel_id=1, source_target_pairs={{16,0},{32,16},{48,32},{64,48},{80,64},{96,80},{112,96},{128,112},... | collective-permute-start | bytes 589832 | tf_op jit(solution)/shard_map/ppermute | solution.py:38
  6.9 13.5 %collective-permute-start.1 = (f32[3,64,256]{2,0,1:T(4,128)S(1)}, f32[3,64,256]{2,0,1:T(4,128)S(1)}, u32[]{:S(2)}, u32[]{:S(2)}) collective-permute-start(f32[3,64,256]{2,0,1:T(4,128)S(1)} %get-tuple-element.168), channel_id=1, source_target_pairs={{0,16},{16,32},{32,48},{48,64},{64,80},{80,96},{96,112},{112,128},... | collective-permute-start | bytes 589832 | tf_op jit(solution)/shard_map/ppermute | solution.py:37
  11.5 8.7 %collective-permute-start.2 = (f32[32,3,256]{2,0,1:T(8,128)S(1)}, f32[32,3,256]{2,0,1:T(8,128)S(1)}, u32[]{:S(2)}, u32[]{:S(2)}) collective-permute-start(f32[32,3,256]{2,0,1:T(8,128)S(1)} %get-tuple-element.171), channel_id=1, source_target_pairs={{1,0},{2,1},{3,2},{4,3},{5,4},{6,5},{7,6},{8,7},{9,8},{10,9},{11,1... | collective-permute-start | bytes 294920 | tf_op jit(solution)/shard_map/ppermute | solution.py:38
  16.6 3.7 %collective-permute-start.3 = (f32[32,3,256]{2,0,1:T(8,128)S(1)}, f32[32,3,256]{2,0,1:T(8,128)S(1)}, u32[]{:S(2)}, u32[]{:S(2)}) collective-permute-start(f32[32,3,256]{2,0,1:T(8,128)S(1)} %get-tuple-element.170), channel_id=1, source_target_pairs={{0,1},{1,2},{2,3},{3,4},{4,5},{5,6},{6,7},{7,8},{8,9},{9,10},{10,1... | collective-permute-start | bytes 294920 | tf_op jit(solution)/shard_map/ppermute | solution.py:37
  39.7 5.3 %collective-permute-start.4 = (f32[3,2,12,32]{3,2,1,0:T(8,128)S(1)}, f32[3,2,12,32]{3,2,1,0:T(8,128)S(1)}, u32[]{:S(2)}, u32[]{:S(2)}) collective-permute-start(f32[3,2,12,32]{3,2,1,0:T(8,128)S(1)} %get-tuple-element.177), channel_id=1, source_target_pairs={{16,0},{32,16},{48,32},{64,48},{80,64},{96,80},{112,96},{128,112},... | collective-permute-start | bytes 27656 | tf_op jit(solution)/shard_map/ppermute | solution.py:22
  41.0 5.2 %collective-permute-start.5 = (f32[3,2,12,32]{3,2,1,0:T(8,128)S(1)}, f32[3,2,12,32]{3,2,1,0:T(8,128)S(1)}, u32[]{:S(2)}, u32[]{:S(2)}) collective-permute-start(f32[3,2,12,32]{3,2,1,0:T(8,128)S(1)} %get-tuple-element.176), channel_id=1, source_target_pairs={{0,16},{16,32},{32,48},{48,64},{64,80},{80,96},{96,112},{112,128},... | collective-permute-start | bytes 27656 | tf_op jit(solution)/shard_map/ppermute | solution.py:22
  46.2 7.4 %collective-permute-start.6 = (f32[3,4,2,32]{3,2,1,0:T(2,128)S(1)}, f32[3,4,2,32]{3,2,1,0:T(2,128)S(1)}, u32[]{:S(2)}, u32[]{:S(2)}) collective-permute-start(f32[3,4,2,32]{3,2,1,0:T(2,128)S(1)} %get-tuple-element.189), channel_id=1, source_target_pairs={{1,0},{2,1},{3,2},{4,3},{5,4},{6,5},{7,6},{8,7},{9,8},{10,9},{11,1... | collective-permute-start | bytes 9224 | tf_op jit(solution)/shard_map/ppermute | solution.py:22
  49.8 4.4 %collective-permute-start.7 = (f32[3,4,2,32]{3,2,1,0:T(2,128)S(1)}, f32[3,4,2,32]{3,2,1,0:T(2,128)S(1)}, u32[]{:S(2)}, u32[]{:S(2)}) collective-permute-start(f32[3,4,2,32]{3,2,1,0:T(2,128)S(1)} %get-tuple-element.188), channel_id=1, source_target_pairs={{0,1},{1,2},{2,3},{3,4},{4,5},{5,6},{6,7},{7,8},{8,9},{9,10},{10,1... | collective-permute-start | bytes 9224 | tf_op jit(solution)/shard_map/ppermute | solution.py:22
  54.3 5.3 %collective-permute-start.8 = (f32[3,2,8,32]{3,2,1,0:T(8,128)S(1)}, f32[3,2,8,32]{3,2,1,0:T(8,128)S(1)}, u32[]{:S(2)}, u32[]{:S(2)}) collective-permute-start(f32[3,2,8,32]{3,2,1,0:T(8,128)S(1)} %get-tuple-element.192), channel_id=1, source_target_pairs={{0,16},{16,32},{32,48},{48,64},{64,80},{80,96},{96,112},{112,128},... | collective-permute-start | bytes 18440 | tf_op jit(solution)/shard_map/ppermute | solution.py:57
  58.2 4.8 %collective-permute-start.9 = (f32[3,2,8,32]{3,2,1,0:T(8,128)S(1)}, f32[3,2,8,32]{3,2,1,0:T(8,128)S(1)}, u32[]{:S(2)}, u32[]{:S(2)}) collective-permute-start(f32[3,2,8,32]{3,2,1,0:T(8,128)S(1)} %get-tuple-element.193), channel_id=1, source_target_pairs={{16,0},{32,16},{48,32},{64,48},{80,64},{96,80},{112,96},{128,112},... | collective-permute-start | bytes 18440 | tf_op jit(solution)/shard_map/ppermute | solution.py:59
  63.1 7.3 %collective-permute-start.10 = (f32[3,8,2,32]{3,2,1,0:T(2,128)S(1)}, f32[3,8,2,32]{3,2,1,0:T(2,128)S(1)}, u32[]{:S(2)}, u32[]{:S(2)}) collective-permute-start(f32[3,8,2,32]{3,2,1,0:T(2,128)S(1)} %get-tuple-element.186), channel_id=1, source_target_pairs={{0,1},{1,2},{2,3},{3,4},{4,5},{5,6},{6,7},{7,8},{8,9},{9,10},{10,1... | collective-permute-start | bytes 18440 | tf_op jit(solution)/shard_map/ppermute | solution.py:57
  68.5 5.1 %collective-permute-start.11 = (f32[3,8,2,32]{3,2,1,0:T(2,128)S(1)}, f32[3,8,2,32]{3,2,1,0:T(2,128)S(1)}, u32[]{:S(2)}, u32[]{:S(2)}) collective-permute-start(f32[3,8,2,32]{3,2,1,0:T(2,128)S(1)} %get-tuple-element.187), channel_id=1, source_target_pairs={{1,0},{2,1},{3,2},{4,3},{5,4},{6,5},{7,6},{8,7},{9,8},{10,9},{11,1... | collective-permute-start | bytes 18440 | tf_op jit(solution)/shard_map/ppermute | solution.py:59
  87.6 7.7 %collective-permute-start.12 = (f32[3,2,12,32]{3,2,1,0:T(8,128)S(1)}, f32[3,2,12,32]{3,2,1,0:T(8,128)S(1)}, u32[]{:S(2)}, u32[]{:S(2)}) collective-permute-start(f32[3,2,12,32]{3,2,1,0:T(8,128)S(1)} %get-tuple-element.175), channel_id=1, source_target_pairs={{16,0},{32,16},{48,32},{64,48},{80,64},{96,80},{112,96},{128,112},... | collective-permute-start | bytes 27656 | tf_op jit(solution)/shard_map/ppermute | solution.py:22
  89.0 7.5 %collective-permute-start.13 = (f32[3,2,12,32]{3,2,1,0:T(8,128)S(1)}, f32[3,2,12,32]{3,2,1,0:T(8,128)S(1)}, u32[]{:S(2)}, u32[]{:S(2)}) collective-permute-start(f32[3,2,12,32]{3,2,1,0:T(8,128)S(1)} %get-tuple-element.174), channel_id=1, source_target_pairs={{0,16},{16,32},{32,48},{48,64},{64,80},{80,96},{96,112},{112,128},... | collective-permute-start | bytes 27656 | tf_op jit(solution)/shard_map/ppermute | solution.py:22
  96.5 5.6 %collective-permute-start.14 = (f32[3,4,2,32]{3,2,1,0:T(2,128)S(1)}, f32[3,4,2,32]{3,2,1,0:T(2,128)S(1)}, u32[]{:S(2)}, u32[]{:S(2)}) collective-permute-start(f32[3,4,2,32]{3,2,1,0:T(2,128)S(1)} %get-tuple-element.185), channel_id=1, source_target_pairs={{1,0},{2,1},{3,2},{4,3},{5,4},{6,5},{7,6},{8,7},{9,8},{10,9},{11,1... | collective-permute-start | bytes 9224 | tf_op jit(solution)/shard_map/ppermute | solution.py:22
  98.5 4.5 %collective-permute-start.15 = (f32[3,4,2,32]{3,2,1,0:T(2,128)S(1)}, f32[3,4,2,32]{3,2,1,0:T(2,128)S(1)}, u32[]{:S(2)}, u32[]{:S(2)}) collective-permute-start(f32[3,4,2,32]{3,2,1,0:T(2,128)S(1)} %get-tuple-element.184), channel_id=1, source_target_pairs={{0,1},{1,2},{2,3},{3,4},{4,5},{5,6},{6,7},{7,8},{8,9},{9,10},{10,1... | collective-permute-start | bytes 9224 | tf_op jit(solution)/shard_map/ppermute | solution.py:22
  162.4 4.9 %collective-permute-start.16 = (f32[3,2,8,32]{3,2,1,0:T(8,128)S(1)}, f32[3,2,8,32]{3,2,1,0:T(8,128)S(1)}, u32[]{:S(2)}, u32[]{:S(2)}) collective-permute-start(f32[3,2,8,32]{3,2,1,0:T(8,128)S(1)} %get-tuple-element.190), channel_id=1, source_target_pairs={{0,16},{16,32},{32,48},{48,64},{64,80},{80,96},{96,112},{112,128},... | collective-permute-start | bytes 18440 | tf_op jit(solution)/shard_map/ppermute | solution.py:57
  166.0 4.6 %collective-permute-start.17 = (f32[3,2,8,32]{3,2,1,0:T(8,128)S(1)}, f32[3,2,8,32]{3,2,1,0:T(8,128)S(1)}, u32[]{:S(2)}, u32[]{:S(2)}) collective-permute-start(f32[3,2,8,32]{3,2,1,0:T(8,128)S(1)} %get-tuple-element.191), channel_id=1, source_target_pairs={{16,0},{32,16},{48,32},{64,48},{80,64},{96,80},{112,96},{128,112},... | collective-permute-start | bytes 18440 | tf_op jit(solution)/shard_map/ppermute | solution.py:59
  170.6 7.5 %collective-permute-start.18 = (f32[3,8,2,32]{3,2,1,0:T(2,128)S(1)}, f32[3,8,2,32]{3,2,1,0:T(2,128)S(1)}, u32[]{:S(2)}, u32[]{:S(2)}) collective-permute-start(f32[3,8,2,32]{3,2,1,0:T(2,128)S(1)} %get-tuple-element.182), channel_id=1, source_target_pairs={{0,1},{1,2},{2,3},{3,4},{4,5},{5,6},{6,7},{7,8},{8,9},{9,10},{10,1... | collective-permute-start | bytes 18440 | tf_op jit(solution)/shard_map/ppermute | solution.py:57
  175.9 5.1 %collective-permute-start.19 = (f32[3,8,2,32]{3,2,1,0:T(2,128)S(1)}, f32[3,8,2,32]{3,2,1,0:T(2,128)S(1)}, u32[]{:S(2)}, u32[]{:S(2)}) collective-permute-start(f32[3,8,2,32]{3,2,1,0:T(2,128)S(1)} %get-tuple-element.183), channel_id=1, source_target_pairs={{1,0},{2,1},{3,2},{4,3},{5,4},{6,5},{7,6},{8,7},{9,8},{10,9},{11,1... | collective-permute-start | bytes 18440 | tf_op jit(solution)/shard_map/ppermute | solution.py:59
  195.1 5.3 %collective-permute-start.20 = (f32[3,2,12,32]{3,2,1,0:T(8,128)S(1)}, f32[3,2,12,32]{3,2,1,0:T(8,128)S(1)}, u32[]{:S(2)}, u32[]{:S(2)}) collective-permute-start(f32[3,2,12,32]{3,2,1,0:T(8,128)S(1)} %get-tuple-element.173), channel_id=1, source_target_pairs={{16,0},{32,16},{48,32},{64,48},{80,64},{96,80},{112,96},{128,112},... | collective-permute-start | bytes 27656 | tf_op jit(solution)/shard_map/ppermute | solution.py:22
  196.4 5.2 %collective-permute-start.21 = (f32[3,2,12,32]{3,2,1,0:T(8,128)S(1)}, f32[3,2,12,32]{3,2,1,0:T(8,128)S(1)}, u32[]{:S(2)}, u32[]{:S(2)}) collective-permute-start(f32[3,2,12,32]{3,2,1,0:T(8,128)S(1)} %get-tuple-element.172), channel_id=1, source_target_pairs={{0,16},{16,32},{32,48},{48,64},{64,80},{80,96},{96,112},{112,128},... | collective-permute-start | bytes 27656 | tf_op jit(solution)/shard_map/ppermute | solution.py:22
  201.6 5.6 %collective-permute-start.22 = (f32[3,4,2,32]{3,2,1,0:T(2,128)S(1)}, f32[3,4,2,32]{3,2,1,0:T(2,128)S(1)}, u32[]{:S(2)}, u32[]{:S(2)}) collective-permute-start(f32[3,4,2,32]{3,2,1,0:T(2,128)S(1)} %get-tuple-element.181), channel_id=1, source_target_pairs={{1,0},{2,1},{3,2},{4,3},{5,4},{6,5},{7,6},{8,7},{9,8},{10,9},{11,1... | collective-permute-start | bytes 9224 | tf_op jit(solution)/shard_map/ppermute | solution.py:22
  203.6 4.5 %collective-permute-start.23 = (f32[3,4,2,32]{3,2,1,0:T(2,128)S(1)}, f32[3,4,2,32]{3,2,1,0:T(2,128)S(1)}, u32[]{:S(2)}, u32[]{:S(2)}) collective-permute-start(f32[3,4,2,32]{3,2,1,0:T(2,128)S(1)} %get-tuple-element.180), channel_id=1, source_target_pairs={{0,1},{1,2},{2,3},{3,4},{4,5},{5,6},{6,7},{7,8},{8,9},{9,10},{10,1... | collective-permute-start | bytes 9224 | tf_op jit(solution)/shard_map/ppermute | solution.py:22
  (4 other events, 45.9 us)
where the time goes:
time: 264 us; the launch traced here: 259 us
  blocking collectives  102 us (39%)
  starting transfers between devices  74.5 us (28%)
  matrix products  33.8 us (13%)
  other arithmetic  20.9 us (8%)
  waiting for transfers between devices  18.5 us (7%)
  between operations  7.86 us (3%)
    psum x8, blocking collectives, by_axis(): return functools.reduce(lax.psum, axes, x)  102 us
    ppermute x12, starting transfers between devices, from_behind(): lax.ppermute(value, axis, [(source, source + steps) for source in range(i...  36.7 us
    ppermute x4, starting transfers between devices, padded_2(): lax.ppermute(tail, axis, [(i, (i + 1) % count) for i in range(ends)])  18.3 us
    ppermute x4, waiting for transfers between devices, padded_2(): lax.ppermute(head, axis, [((i + 1) % count, i) for i in range(ends)])  12.9 us
    dot_general x2, matrix products, decode(): return jnp.einsum('za,cayx->czyx', along_z, inner, precision=hp)  12.4 us
    dot_general x3, matrix products, encode(): inner = jnp.einsum('za,czyx->cayx', along_z, volume, precision=hp)  12.2 us
    another operation x2, other arithmetic, shards(): jnp.stack([derivative(framed[:, 3:-3, 3:-3], 0), derivative(framed[3:-3,...  8.44 us
    ppermute x4, starting transfers between devices, padded_2(): lax.ppermute(head, axis, [((i + 1) % count, i) for i in range(ends)])  6.68 us
  transfers between devices with their start and end apart: 24, of which 10 were waited for; matrix products, arithmetic and copies ran while one was open for 1% of the time, Pallas kernels for 0%

commit v1 on v0

v1 whole, which is shorter than its diff:
```python
import functools

import jax
import jax.numpy as jnp
import numpy as np
from jax import lax
from jax.experimental import pallas as pl
from jax.experimental.pallas import tpu as pltpu
from jax.sharding import PartitionSpec as P

SPACING = 8
DAMPING = 8.0
CZ, CY, NX = 32, 64, 256
CA, CB, CE = 4, 8, 32
A, B, LANES = 7, 16, 128
BP = 12
ROWS = A * BP
CHUNK = 256
STEPS = CZ * CY // CHUNK
MESH = pl.DeviceIdType.MESH
F32, BF16 = jnp.float32, jnp.bfloat16


def basis_matrix(count, columns, offset):
    voxel = np.arange(count)
    cell = voxel // SPACING
    frac = (voxel % SPACING + 0.5) / SPACING
    other = 1.0 - frac
    weights = (
        other**3 / 6.0,
        (3.0 * frac**3 - 6.0 * frac**2 + 4.0) / 6.0,
        (-3.0 * frac**3 + 3.0 * frac**2 + 3.0 * frac + 1.0) / 6.0,
        frac**3 / 6.0,
    )
    matrix = np.zeros((count, columns))
    for tap in range(4):
        for v in range(count):
            column = cell[v] - 1 + tap + offset
            if 0 <= column < columns:
                matrix[v, column] += weights[tap][v]
    return matrix


def halves(x):
    x = np.asarray(x, np.float32)
    high = x.astype(jnp.bfloat16)
    low = (x - high.astype(np.float32)).astype(jnp.bfloat16)
    return high, low


def constants():
    bz = basis_matrix(CZ, A, 1)
    by = basis_matrix(CY, B, 1)
    bx = basis_matrix(NX, CE, 0)
    kron12 = np.einsum("za,yb->zyab", bz, by[:, :BP]).reshape(CZ * CY, ROWS)
    high, low = halves(kron12)
    pad = np.zeros((CZ * CY, 256 - 3 * ROWS), jnp.bfloat16)
    kd = np.concatenate([high, high, low, pad], axis=1)
    kron16 = np.einsum("za,yb->abzy", bz, by).reshape(A * B, CZ * CY)
    ke = np.concatenate(halves(kron16), axis=0)
    spread = np.zeros((LANES, 3 * NX))
    for c in range(3):
        spread[c * CE : (c + 1) * CE, c * NX : (c + 1) * NX] = bx.T
    high, low = halves(spread)
    bxd = np.concatenate([high, high, low], axis=0)
    gather = np.concatenate([high.T, low.T], axis=1)
    bxe = np.concatenate([gather, gather], axis=0)
    dx = np.zeros((NX, NX))
    for step, weight in ((1, 45.0), (2, -9.0), (3, 1.0)):
        for v in range(NX):
            if v + step < NX:
                dx[v + step, v] = weight
            if v - step >= 0:
                dx[v - step, v] = -weight
    dx = np.concatenate([dx, dx], axis=0).astype(jnp.bfloat16)
    return kd, ke, bxd, bxe, dx


def split(x):
    high = x.astype(BF16)
    return high, (x - high.astype(F32)).astype(BF16)


def dot(a, b):
    return jnp.dot(a, b, preferred_element_type=F32)


def kernel(nz, ny, fixed, moving, kd_h, ke_h, bxd_h, bxe_h, dx_h, upd, res,
           fv, mv, mp, fl, ml, fh, mh, yls, yhs, zlr, zhr, ylr, yhr,
           g, s0, sw, u, cs, p3, kd, ke, bxd, bxe, dx,
           enc, rz, ry, rc, ars, arr,
           lsem, hss, hrs, xss, xrs, ass, arsem):
    d = lax.axis_index("gz")
    e = lax.axis_index("gy")
    up, down = lax.rem(d + 1, nz), lax.rem(d + nz - 1, nz)
    right, left = lax.rem(e + 1, ny), lax.rem(e + ny - 1, ny)

    barrier = pltpu.get_barrier_semaphore()

    def greet_y(k, carry):
        pl.semaphore_signal(barrier, inc=1, device_id=(d, lax.rem(e + k, ny)), device_id_type=MESH)
        return carry

    def greet_z(k, carry):
        pl.semaphore_signal(barrier, inc=1, device_id=(lax.rem(d + k, nz), e), device_id_type=MESH)
        return carry

    for z in (up, down):
        for y in (right, left):
            pl.semaphore_signal(barrier, inc=1, device_id=(z, y), device_id_type=MESH)
    lax.fori_loop(1, ny, greet_y, 0)
    lax.fori_loop(1, nz, greet_z, 0)

    def local(k, src, dst):
        copy = pltpu.make_async_copy(src, dst, lsem.at[k])
        copy.start()
        return copy

    faces_z = [
        local(0, fixed.at[pl.ds(0, 3)], fv.at[pl.ds(0, 3)]),
        local(1, moving.at[pl.ds(0, 3)], mv.at[pl.ds(0, 3)]),
        local(2, fixed.at[pl.ds(CZ - 3, 3)], fv.at[pl.ds(CZ - 3, 3)]),
        local(3, moving.at[pl.ds(CZ - 3, 3)], mv.at[pl.ds(CZ - 3, 3)]),
    ]
    faces_y = [
        local(4, fixed.at[:, pl.ds(0, 8)], fl),
        local(5, moving.at[:, pl.ds(0, 8)], ml),
        local(6, fixed.at[:, pl.ds(CY - 8, 8)], fh),
        local(7, moving.at[:, pl.ds(CY - 8, 8)], mh),
    ]
    rest = [
        local(8, fixed.at[pl.ds(3, CZ - 6)], fv.at[pl.ds(3, CZ - 6)]),
        local(9, moving.at[pl.ds(3, CZ - 6)], mv.at[pl.ds(3, CZ - 6)]),
        local(10, dx_h, dx),
        local(11, bxe_h, bxe),
    ]
    later = [local(12, ke_h, ke), local(13, bxd_h, bxd), local(14, kd_h, kd)]

    def remote(src, dst, send, recv, z, y):
        return pltpu.make_async_remote_copy(
            src_ref=src, dst_ref=dst, send_sem=send, recv_sem=recv, device_id=(z, y), device_id_type=MESH
        )

    for copy in faces_z:
        copy.wait()
    for z in (0, 1, 2, CZ - 3, CZ - 2, CZ - 1):
        mp[z + 3, 8 : 8 + CY, :] = 0.5 * (fv[z] + mv[z])
    for copy in faces_y:
        copy.wait()
    yls[...] = 0.5 * (fl[:, 0:4, :] + ml[:, 0:4, :])
    yhs[...] = 0.5 * (fh[:, 4:8, :] + mh[:, 4:8, :])
    pl.semaphore_wait(barrier, 4 + (ny - 1) + (nz - 1))
    halo = [
        remote(mp.at[pl.ds(CZ, 3), pl.ds(8, CY)], zlr, hss.at[0], hrs.at[0], up, e),
        remote(mp.at[pl.ds(3, 3), pl.ds(8, CY)], zhr, hss.at[1], hrs.at[1], down, e),
        remote(yhs, ylr, hss.at[2], hrs.at[2], d, right),
        remote(yls, yhr, hss.at[3], hrs.at[3], d, left),
    ]
    for copy in halo:
        copy.start()

    has_down = jnp.where(d > 0, 1.0, 0.0).astype(F32)
    has_up = jnp.where(d < nz - 1, 1.0, 0.0).astype(F32)
    has_left = jnp.where(e > 0, 1.0, 0.0).astype(F32)
    has_right = jnp.where(e < ny - 1, 1.0, 0.0).astype(F32)
    p3[...] = jnp.zeros_like(p3)

    for copy in rest:
        copy.wait()

    def fill(z, carry):
        mp[z + 3, 8 : 8 + CY, :] = 0.5 * (fv[z] + mv[z])
        return carry

    lax.fori_loop(3, CZ - 3, fill, 0)

    halo[2].wait_recv()
    mp[3 : CZ + 3, 4:8, :] = has_left * ylr[...]
    halo[3].wait_recv()
    mp[3 : CZ + 3, 8 + CY : 12 + CY, :] = has_right * yhr[...]

    def gather_x(volume, j):
        parts = [split(v) for v in volume]
        total = None
        for c in range(3):
            weights = bxe[pl.ds(c * NX, NX), :]
            for part in parts[c]:
                term = dot(part, weights)
                total = term if total is None else total + term
        high, low = split(total[:, :LANES] + total[:, LANES:])
        rows = pl.ds(pl.multiple_of(j * CHUNK, CHUNK), CHUNK)
        u[rows, 0:LANES] = high
        u[rows, LANES : 2 * LANES] = low

    def first(j):
        z = j * 4
        rows = pl.ds(pl.multiple_of(j * CHUNK, CHUNK), CHUNK)

        def along_z(k):
            return mp[pl.ds(z + 3 + k, 4), 8 : 8 + CY, :]

        def along_y(k):
            return mp[pl.ds(z + 3, 4), 8 + k : 8 + k + CY, :]

        def difference(part):
            return 45.0 * (part(1) - part(-1)) - 9.0 * (part(2) - part(-2)) + (part(3) - part(-3))

        centre = along_z(0).reshape(CHUNK, NX)
        high, low = split(centre)
        sixtieth = 1.0 / 60.0
        slopes = (
            difference(along_z).reshape(CHUNK, NX),
            difference(along_y).reshape(CHUNK, NX),
            dot(high, dx[0:NX, :]) + dot(low, dx[NX : 2 * NX, :]),
        )
        mismatch = (fv[pl.ds(z, 4)] - mv[pl.ds(z, 4)]).reshape(CHUNK, NX)
        volume = []
        for c in range(3):
            rounded = (slopes[c] * sixtieth).astype(BF16)
            g[c, rows, :] = rounded
            volume.append(rounded.astype(F32) * mismatch)
        gather_x(volume, j)

    def first_inner(j, carry):
        first(j)
        return carry

    lax.fori_loop(1, STEPS - 1, first_inner, 0)
    halo[0].wait_recv()
    mp[0:3, 8 : 8 + CY, :] = has_down * zlr[...]
    halo[1].wait_recv()
    mp[CZ + 3 : CZ + 6, 8 : 8 + CY, :] = has_up * zhr[...]

    def first_outer(t, carry):
        first(t * (STEPS - 1))
        return carry

    lax.fori_loop(0, 2, first_outer, 0)
    for copy in later:
        copy.wait()

    row = lax.broadcasted_iota(jnp.int32, (1, 8, LANES), 1)
    low_rows = jnp.where(row < 3, 1.0, 0.0).astype(F32)
    from_right = has_right * low_rows
    pa = lax.broadcasted_iota(jnp.int32, (A, B, LANES), 0) + (d * CA - 1)
    pb = lax.broadcasted_iota(jnp.int32, (A, B, LANES), 1) + (e * CB - 1)
    ia = lax.broadcasted_iota(jnp.int32, (A, B, LANES), 0)
    ib = lax.broadcasted_iota(jnp.int32, (A, B, LANES), 1)
    inside = (pa >= 0) & (pa < nz * CA) & (pb >= 0) & (pb < ny * CB) & (ib < 11)
    inside = jnp.where(inside, 1.0, 0.0).astype(F32)
    own = jnp.where((ia >= 1) & (ia < 1 + CA) & (ib >= 1) & (ib < 1 + CB), 1.0, 0.0).astype(F32)

    def exchange(k):
        both = dot(ke[...], u[...])
        half = A * B
        total = both[:half, :LANES] + both[half:, :LANES] + both[:half, LANES:]
        enc[k] = total.reshape(A, B, LANES)
        src = enc.at[k]
        top, bottom = pl.ds(A - 3, 3), pl.ds(0, 3)
        after, before = pl.ds(8, 8), pl.ds(0, 8)
        copies = [
            remote(src.at[top, after], rc.at[k, 0], xss.at[k, 0], xrs.at[k, 0], up, right),
            remote(src.at[top, before], rc.at[k, 1], xss.at[k, 1], xrs.at[k, 1], up, left),
            remote(src.at[bottom, after], rc.at[k, 2], xss.at[k, 2], xrs.at[k, 2], down, right),
            remote(src.at[bottom, before], rc.at[k, 3], xss.at[k, 3], xrs.at[k, 3], down, left),
            remote(src.at[top], rz.at[k, 0], xss.at[k, 4], xrs.at[k, 4], up, e),
            remote(src.at[bottom], rz.at[k, 1], xss.at[k, 5], xrs.at[k, 5], down, e),
            remote(src.at[:, after], ry.at[k, 0], xss.at[k, 6], xrs.at[k, 6], d, right),
            remote(src.at[:, before], ry.at[k, 1], xss.at[k, 7], xrs.at[k, 7], d, left),
        ]
        for copy in copies:
            copy.start()
        return copies

    def collect(k, copies):
        for copy in copies:
            copy.wait_recv()
        left_half = enc[k, :, 0:8, :] + has_left * ry[k, 0]
        right_half = enc[k, :, 8:16, :] + from_right * ry[k, 1]
        below = has_down * rz[k, 0]
        above = has_up * rz[k, 1]
        left_low = below[:, 0:8] + (has_down * has_left) * rc[k, 0]
        right_low = below[:, 8:16] + has_down * from_right * rc[k, 1]
        left_high = above[:, 0:8] + (has_up * has_left) * rc[k, 2]
        right_high = above[:, 8:16] + has_up * from_right * rc[k, 3]

        def stack(middle, low, high):
            return jnp.concatenate([middle[0:3] + low, middle[3:4], middle[4:7] + high], axis=0)

        whole = jnp.concatenate(
            [stack(left_half, left_low, left_high), stack(right_half, right_low, right_high)], axis=1
        )
        return whole * inside

    def spread_x(control):
        for t in range(3):
            for a in range(A):
                p3[t * ROWS + a * BP : t * ROWS + (a + 1) * BP, :] = control[a, 0:BP, :]
        high, low = split(p3[...])
        wide = dot(jnp.concatenate([high, low, high], axis=1), bxd[...])
        index = lax.broadcasted_iota(jnp.int32, (256, 3 * NX), 0)
        middle = (index >= ROWS) & (index < 2 * ROWS)
        rounded = wide.astype(BF16).astype(F32)
        cs[...] = jnp.where(middle, wide - rounded, rounded).astype(BF16)

    def apply(dst, j, carry):
        rows = pl.ds(pl.multiple_of(j * CHUNK, CHUNK), CHUNK)
        field = dot(kd[rows, :], cs[...])
        slopes = [g[c, rows, :].astype(F32) for c in range(3)]
        s = slopes[0] * field[:, 0:NX]
        s = s + slopes[1] * field[:, NX : 2 * NX]
        s = s + slopes[2] * field[:, 2 * NX : 3 * NX]
        dst[rows, :] = s
        gather_x([slopes[c] * s for c in range(3)], j)
        return carry + jnp.sum((s * s).reshape(CHUNK // 8, 8, NX), axis=0)

    def fold(x):
        total = jnp.sum(x, axis=0, keepdims=True)
        return total[:, 0:LANES] + total[:, LANES : 2 * LANES]

    def tile_sum(x):
        return jnp.sum(jnp.sum(x, axis=0), axis=0, keepdims=True)

    def reduce_start(i, stage, value):
        me, count = (e, ny) if stage == 0 else (d, nz)
        ars[i, stage] = value
        arr[i, stage, me] = value

        def send(k, carry):
            other = lax.rem(me + k, count)
            z, y = (d, other) if stage == 0 else (other, e)
            remote(ars.at[i, stage], arr.at[i, stage, me], ass.at[i, stage, k], arsem.at[i, stage, me], z, y).start()
            return carry

        lax.fori_loop(1, count, send, 0)

    def reduce_end(i, stage):
        me, count = (e, ny) if stage == 0 else (d, nz)

        def take(k, carry):
            other = lax.rem(me + count - k, count)
            remote(ars.at[i, stage], arr.at[i, stage, other], ass.at[i, stage, k], arsem.at[i, stage, other], d, e).wait_recv()
            return carry

        lax.fori_loop(1, count, take, 0)
        return jnp.sum(arr[i, stage], axis=0)

    def scalars(i):
        total = reduce_end(i, 1)
        total = jnp.sum(total, axis=1, keepdims=True)
        return total[0:1], total[1:2]

    copies0 = exchange(0)
    r0 = collect(0, copies0)
    spread_x(r0)
    square = tile_sum(r0 * r0 * own)
    zero = jnp.zeros((8, NX), F32)
    energy = fold(lax.fori_loop(0, STEPS, functools.partial(apply, s0), zero))
    copies1 = exchange(1)
    reduce_start(0, 0, jnp.concatenate([square, energy], axis=0))
    w0 = collect(1, copies1) + DAMPING * r0
    reduce_start(0, 1, reduce_end(0, 0))
    spread_x(w0)
    lax.fori_loop(0, STEPS, functools.partial(apply, sw), zero)
    copies2 = exchange(2)
    rr0, energy0 = scalars(0)
    alpha0 = rr0 / (energy0 + DAMPING * rr0)
    r1 = r0 - alpha0.reshape(1, 1, 1) * w0

    def combine(j, carry):
        rows = pl.ds(pl.multiple_of(j * CHUNK, CHUNK), CHUNK)
        s = s0[rows, :] - alpha0 * sw[rows, :]
        return carry + jnp.sum((s * s).reshape(CHUNK // 8, 8, NX), axis=0)

    energy = fold(lax.fori_loop(0, STEPS, combine, zero))
    reduce_start(1, 0, jnp.concatenate([tile_sum(r1 * r1 * own), energy], axis=0))
    v = collect(2, copies2) + DAMPING * w0
    reduce_start(1, 1, reduce_end(1, 0))
    rr1, energy1 = scalars(1)
    beta = rr1 / rr0
    product = energy1 + DAMPING * rr1 - beta * rr1 / alpha0
    alpha1 = rr1 / product
    alpha0, alpha1, beta = (x.reshape(1, 1, 1) for x in (alpha0, alpha1, beta))
    direction = r1 + beta * r0
    along = w0 - alpha0 * v + beta * w0
    update = alpha0 * r0 + alpha1 * direction
    residual = r1 - alpha1 * along
    for c in range(3):
        upd[c] = update[1 : 1 + CA, 1 : 1 + CB, c * CE : (c + 1) * CE]
        res[c] = residual[1 : 1 + CA, 1 : 1 + CB, c * CE : (c + 1) * CE]

    for copy in halo + copies0 + copies1 + copies2:
        copy.wait_send()
    for i in range(2):
        for stage in range(2):
            count = ny if stage == 0 else nz

            def sent(k, carry):
                remote(ars.at[i, stage], arr.at[i, stage, 0], ass.at[i, stage, k], arsem.at[i, stage, 0], d, e).wait_send()
                return carry

            lax.fori_loop(1, count, sent, 0)


def solution(mesh):
    nz, ny = mesh.shape["gz"], mesh.shape["gy"]
    tables = constants()
    count = max(nz, ny)
    vmem = pltpu.VMEM
    dma = pltpu.SemaphoreType.DMA
    scratch = [
        vmem((CZ, CY, NX), F32), vmem((CZ, CY, NX), F32),
        vmem((CZ + 6, CY + 16, NX), F32),
        vmem((CZ, 8, NX), F32), vmem((CZ, 8, NX), F32), vmem((CZ, 8, NX), F32), vmem((CZ, 8, NX), F32),
        vmem((CZ, 4, NX), F32), vmem((CZ, 4, NX), F32),
        vmem((3, CY, NX), F32), vmem((3, CY, NX), F32),
        vmem((CZ, 4, NX), F32), vmem((CZ, 4, NX), F32),
        vmem((3, CZ * CY, NX), BF16),
        vmem((CZ * CY, NX), F32), vmem((CZ * CY, NX), F32),
        vmem((CZ * CY, 2 * LANES), BF16),
        vmem((256, 3 * NX), BF16),
        vmem((256, LANES), F32),
    ] + [vmem(t.shape, BF16) for t in tables] + [
        vmem((3, A, B, LANES), F32),
        vmem((3, 2, 3, B, LANES), F32),
        vmem((3, 2, A, 8, LANES), F32),
        vmem((3, 4, 3, 8, LANES), F32),
        vmem((2, 2, 2, LANES), F32),
        vmem((2, 2, count, 2, LANES), F32),
        dma((15,)), dma((4,)), dma((4,)), dma((3, 8)), dma((3, 8)), dma((2, 2, count)), dma((2, 2, count)),
    ]
    out = jax.ShapeDtypeStruct((3, CA, CB, CE), F32)
    call = pl.pallas_call(
        functools.partial(kernel, nz, ny),
        out_shape=(out, out),
        in_specs=[pl.BlockSpec(memory_space=pl.ANY)] * 7,
        out_specs=(pl.BlockSpec(memory_space=pltpu.VMEM), pl.BlockSpec(memory_space=pltpu.VMEM)),
        scratch_shapes=scratch,
        compiler_params=pltpu.CompilerParams(collective_id=0, has_side_effects=True, vmem_limit_bytes=56 * 1024 * 1024),
        name="cg_step",
    )

    def shards(fixed, moving):
        return call(fixed, moving, *[jnp.asarray(t) for t in tables])

    return jax.shard_map(
        shards,
        mesh=mesh,
        in_specs=(P("gz", "gy", None), P("gz", "gy", None)),
        out_specs=(P(None, "gz", "gy", None), P(None, "gz", "gy", None)),
        check_vma=False,
    )
```

time: 264 us -> 62.5 us (0.24); the launches traced: 259 us -> 62.3 us
  blocking collectives: 102 us -> 0 us
  starting transfers between devices: 74.5 us -> 0 us
  Pallas kernels: 0 us -> 58.8 us
  matrix products: 33.8 us -> 0 us
  other arithmetic: 20.9 us -> 0 us
  waiting for transfers between devices: 18.5 us -> 0 us
  between operations: 7.86 us -> 0.64 us
    psum x8 -> x0, blocking collectives: 102 us -> none  [by_axis(): return functools.reduce(lax.psum, axes, x)]
    ppermute x24 -> x0, starting transfers between devices: 74.5 us -> none  [the longest x12 36.7 us: from_behind(): lax.ppermute(value, axis, [(source, source + steps) for source in range(i...]
    pallas_call x0 -> x1, Pallas kernels: none -> 58.8 us  [shards(): return call(fixed, moving, *[jnp.asarray(t) for t in tables])]
    dot_general x15 -> x0, matrix products: 33.8 us -> none  [the longest x2 12.4 us: decode(): return jnp.einsum('za,cayx->czyx', along_z, inner, precision=hp)]
    ppermute x24 -> x0, waiting for transfers between devices: 18.5 us -> none  [the longest x4 12.9 us: padded_2(): lax.ppermute(head, axis, [((i + 1) % count, i) for i in range(ends)])]
    another operation x2 -> x0, other arithmetic: 8.44 us -> none  [shards(): jnp.stack([derivative(framed[:, 3:-3, 3:-3], 0), derivative(framed[3:-3,...]
    concatenate x2 -> x0, other arithmetic: 4.97 us -> none  [with_halo(): jnp.concatenate([jnp.pad(low, around), x, jnp.pad(high, around)], axis=dim)]
    mul x1 -> x0, other arithmetic: 4.81 us -> none  [shards(): mean = 0.5 * (fixed + moving)]
  transfers between devices with their start and end apart: 24 -> 0, of which waited for: 10 -> 0; matrix products, arithmetic and copies ran while one was open for 1% -> 0% of each run, Pallas kernels for 0% -> 0%
where the time goes in v1:
time: 62.5 us; the launch traced here: 62.3 us
  Pallas kernels  58.8 us (94%)
  local copies, waits for them, and re-layouts  2.84 us (5%)
  between operations  0.64 us (1%)
    pallas_call x1, Pallas kernels, shards(): return call(fixed, moving, *[jnp.asarray(t) for t in tables])  58.8 us
    unnamed x2, local copies, waits for them, and re-layouts  2.84 us

profile of v1, /device:TPU:1, one launch (start us, length us, event | category | flops | bytes accessed | tf_op | source)
XLA Modules:
  0.0 62.3 jit_solution(11808175402770823982)
XLA Ops:
  0.6 58.8 %cg_step.1 = (f32[3,4,8,32]{3,2,1,0:T(8,128)}, f32[3,4,8,32]{3,2,1,0:T(8,128)}) custom-call(f32[32,64,256]{2,1,0:T(8,128)} %fixed.1, f32[32,64,256]{2,1,0:T(8,128)} %moving.1, bf16[2048,256]{1,0:T(8,128)(2,1)} %constant.10.clone.kd_h, bf16[224,2048]{1,0:T(8,128)(2,1)} %constant.11.clone.ke_h, bf16[384,768]{1,0:T(8,128)(2,1)} %constant.12.clone.bxd_h, ...), custom_call_target="tpu_custom_call" | custom-call | tf_op jit(solution)/shard_map/cg_step/pallas_call | solution.py:444
  59.5 1.4 %copy.11 = f32[3,4,8,32]{3,2,1,0:T(8,128)} copy(f32[3,4,8,32]{3,2,1,0:T(8,128)} %get-tuple-element.4) | data formatting | bytes 24576
  60.9 1.4 %copy.12 = f32[3,4,8,32]{3,2,1,0:T(8,128)} copy(f32[3,4,8,32]{3,2,1,0:T(8,128)} %get-tuple-element.5) | data formatting | bytes 24576

commit v2 on v1

--- a/solution.py
+++ b/solution.py
@@ -15,8 +15,10 @@
 A, B, LANES = 7, 16, 128
 BP = 12
 ROWS = A * BP
-CHUNK = 256
+CHUNK = 1024
 STEPS = CZ * CY // CHUNK
+INNER = 8
+OUTER = 4
 MESH = pl.DeviceIdType.MESH
 F32, BF16 = jnp.float32, jnp.bfloat16
 
@@ -62,9 +64,8 @@
     for c in range(3):
         spread[c * CE : (c + 1) * CE, c * NX : (c + 1) * NX] = bx.T
     high, low = halves(spread)
-    bxd = np.concatenate([high, high, low], axis=0)
-    gather = np.concatenate([high.T, low.T], axis=1)
-    bxe = np.concatenate([gather, gather], axis=0)
+    bxd = np.concatenate([high, low], axis=0)
+    bxe = np.concatenate([high.T, low.T], axis=1)
     dx = np.zeros((NX, NX))
     for step, weight in ((1, 45.0), (2, -9.0), (3, 1.0)):
         for v in range(NX):
@@ -72,8 +73,7 @@
                 dx[v + step, v] = weight
             if v - step >= 0:
                 dx[v - step, v] = -weight
-    dx = np.concatenate([dx, dx], axis=0).astype(jnp.bfloat16)
-    return kd, ke, bxd, bxe, dx
+    return kd, ke, bxd, bxe, dx.astype(jnp.bfloat16)
 
 
 def split(x):
@@ -87,8 +87,8 @@
 
 def kernel(nz, ny, fixed, moving, kd_h, ke_h, bxd_h, bxe_h, dx_h, upd, res,
            fv, mv, mp, fl, ml, fh, mh, yls, yhs, zlr, zhr, ylr, yhr,
-           g, s0, sw, u, cs, p3, kd, ke, bxd, bxe, dx,
-           enc, rz, ry, rc, ars, arr,
+           g, u, cs, p3, tot, kd, ke, bxd, bxe, dx,
+           enc, yst, rz, ry, rc, ars, arr,
            lsem, hss, hrs, xss, xrs, ass, arsem):
     d = lax.axis_index("gz")
     e = lax.axis_index("gy")
@@ -134,7 +134,6 @@
         local(10, dx_h, dx),
         local(11, bxe_h, bxe),
     ]
-    later = [local(12, ke_h, ke), local(13, bxd_h, bxd), local(14, kd_h, kd)]
 
     def remote(src, dst, send, recv, z, y):
         return pltpu.make_async_remote_copy(
@@ -167,6 +166,7 @@
 
     for copy in rest:
         copy.wait()
+    later = [local(12, ke_h, ke), local(13, bxd_h, bxd), local(14, kd_h, kd)]
 
     def fill(z, carry):
         mp[z + 3, 8 : 8 + CY, :] = 0.5 * (fv[z] + mv[z])
@@ -179,67 +179,62 @@
     halo[3].wait_recv()
     mp[3 : CZ + 3, 8 + CY : 12 + CY, :] = has_right * yhr[...]
 
-    def gather_x(volume, j):
-        parts = [split(v) for v in volume]
+    def gather_x(volume, rows):
         total = None
         for c in range(3):
-            weights = bxe[pl.ds(c * NX, NX), :]
-            for part in parts[c]:
-                term = dot(part, weights)
-                total = term if total is None else total + term
+            term = dot(volume[c].astype(BF16), bxe[c * NX : (c + 1) * NX, :])
+            total = term if total is None else total + term
         high, low = split(total[:, :LANES] + total[:, LANES:])
-        rows = pl.ds(pl.multiple_of(j * CHUNK, CHUNK), CHUNK)
         u[rows, 0:LANES] = high
         u[rows, LANES : 2 * LANES] = low
 
-    def first(j):
-        z = j * 4
-        rows = pl.ds(pl.multiple_of(j * CHUNK, CHUNK), CHUNK)
+    def first(z, layers):
+        count = layers * CY
+        rows = pl.ds(pl.multiple_of(z * CY, CY * OUTER), count)
 
         def along_z(k):
-            return mp[pl.ds(z + 3 + k, 4), 8 : 8 + CY, :]
+            return mp[pl.ds(z + 3 + k, layers), 8 : 8 + CY, :]
 
         def along_y(k):
-            return mp[pl.ds(z + 3, 4), 8 + k : 8 + k + CY, :]
+            return mp[pl.ds(z + 3, layers), 8 + k : 8 + k + CY, :]
 
         def difference(part):
             return 45.0 * (part(1) - part(-1)) - 9.0 * (part(2) - part(-2)) + (part(3) - part(-3))
 
-        centre = along_z(0).reshape(CHUNK, NX)
-        high, low = split(centre)
+        high, low = split(along_z(0).reshape(count, NX))
         sixtieth = 1.0 / 60.0
         slopes = (
-            difference(along_z).reshape(CHUNK, NX),
-            difference(along_y).reshape(CHUNK, NX),
-            dot(high, dx[0:NX, :]) + dot(low, dx[NX : 2 * NX, :]),
+            difference(along_z).reshape(count, NX),
+            difference(along_y).reshape(count, NX),
+            dot(high, dx[...]) + dot(low, dx[...]),
         )
-        mismatch = (fv[pl.ds(z, 4)] - mv[pl.ds(z, 4)]).reshape(CHUNK, NX)
+        mismatch = (fv[pl.ds(z, layers)] - mv[pl.ds(z, layers)]).reshape(count, NX)
         volume = []
         for c in range(3):
             rounded = (slopes[c] * sixtieth).astype(BF16)
             g[c, rows, :] = rounded
             volume.append(rounded.astype(F32) * mismatch)
-        gather_x(volume, j)
-
-    def first_inner(j, carry):
-        first(j)
+        gather_x(volume, rows)
+
+    def first_inner(t, carry):
+        first(OUTER + t * INNER, INNER)
         return carry
 
-    lax.fori_loop(1, STEPS - 1, first_inner, 0)
+    lax.fori_loop(0, (CZ - 2 * OUTER) // INNER, first_inner, 0)
     halo[0].wait_recv()
     mp[0:3, 8 : 8 + CY, :] = has_down * zlr[...]
     halo[1].wait_recv()
     mp[CZ + 3 : CZ + 6, 8 : 8 + CY, :] = has_up * zhr[...]
 
     def first_outer(t, carry):
-        first(t * (STEPS - 1))
+        first(t * (CZ - OUTER), OUTER)
         return carry
 
     lax.fori_loop(0, 2, first_outer, 0)
     for copy in later:
         copy.wait()
 
-    row = lax.broadcasted_iota(jnp.int32, (1, 8, LANES), 1)
+    row = lax.broadcasted_iota(jnp.int32, (1, 4, LANES), 1)
     low_rows = jnp.where(row < 3, 1.0, 0.0).astype(F32)
     from_right = has_right * low_rows
     pa = lax.broadcasted_iota(jnp.int32, (A, B, LANES), 0) + (d * CA - 1)
@@ -254,19 +249,21 @@
         both = dot(ke[...], u[...])
         half = A * B
         total = both[:half, :LANES] + both[half:, :LANES] + both[:half, LANES:]
-        enc[k] = total.reshape(A, B, LANES)
-        src = enc.at[k]
+        total = total.reshape(A, B, LANES)
+        enc[k] = total
+        yst[k, 0] = total[:, 8:12]
+        yst[k, 1] = total[:, 0:4]
+        src, after, before = enc.at[k], yst.at[k, 0], yst.at[k, 1]
         top, bottom = pl.ds(A - 3, 3), pl.ds(0, 3)
-        after, before = pl.ds(8, 8), pl.ds(0, 8)
         copies = [
-            remote(src.at[top, after], rc.at[k, 0], xss.at[k, 0], xrs.at[k, 0], up, right),
-            remote(src.at[top, before], rc.at[k, 1], xss.at[k, 1], xrs.at[k, 1], up, left),
-            remote(src.at[bottom, after], rc.at[k, 2], xss.at[k, 2], xrs.at[k, 2], down, right),
-            remote(src.at[bottom, before], rc.at[k, 3], xss.at[k, 3], xrs.at[k, 3], down, left),
+            remote(after.at[top], rc.at[k, 0], xss.at[k, 0], xrs.at[k, 0], up, right),
+            remote(before.at[top], rc.at[k, 1], xss.at[k, 1], xrs.at[k, 1], up, left),
+            remote(after.at[bottom], rc.at[k, 2], xss.at[k, 2], xrs.at[k, 2], down, right),
+            remote(before.at[bottom], rc.at[k, 3], xss.at[k, 3], xrs.at[k, 3], down, left),
             remote(src.at[top], rz.at[k, 0], xss.at[k, 4], xrs.at[k, 4], up, e),
             remote(src.at[bottom], rz.at[k, 1], xss.at[k, 5], xrs.at[k, 5], down, e),
-            remote(src.at[:, after], ry.at[k, 0], xss.at[k, 6], xrs.at[k, 6], d, right),
-            remote(src.at[:, before], ry.at[k, 1], xss.at[k, 7], xrs.at[k, 7], d, left),
+            remote(after, ry.at[k, 0], xss.at[k, 6], xrs.at[k, 6], d, right),
+            remote(before, ry.at[k, 1], xss.at[k, 7], xrs.at[k, 7], d, left),
         ]
         for copy in copies:
             copy.start()
@@ -275,43 +272,36 @@
     def collect(k, copies):
         for copy in copies:
             copy.wait_recv()
-        left_half = enc[k, :, 0:8, :] + has_left * ry[k, 0]
-        right_half = enc[k, :, 8:16, :] + from_right * ry[k, 1]
-        below = has_down * rz[k, 0]
-        above = has_up * rz[k, 1]
-        left_low = below[:, 0:8] + (has_down * has_left) * rc[k, 0]
-        right_low = below[:, 8:16] + has_down * from_right * rc[k, 1]
-        left_high = above[:, 0:8] + (has_up * has_left) * rc[k, 2]
-        right_high = above[:, 8:16] + has_up * from_right * rc[k, 3]
-
-        def stack(middle, low, high):
-            return jnp.concatenate([middle[0:3] + low, middle[3:4], middle[4:7] + high], axis=0)
-
-        whole = jnp.concatenate(
-            [stack(left_half, left_low, left_high), stack(right_half, right_low, right_high)], axis=1
-        )
-        return whole * inside
+        tot[...] = enc[k]
+        tot[0:3] += has_down * rz[k, 0]
+        tot[4:7] += has_up * rz[k, 1]
+        tot[:, 0:4] += has_left * ry[k, 0]
+        tot[:, 8:12] += from_right * ry[k, 1]
+        tot[0:3, 0:4] += (has_down * has_left) * rc[k, 0]
+        tot[0:3, 8:12] += has_down * from_right * rc[k, 1]
+        tot[4:7, 0:4] += (has_up * has_left) * rc[k, 2]
+        tot[4:7, 8:12] += has_up * from_right * rc[k, 3]
+        return tot[...] * inside
 
     def spread_x(control):
         for t in range(3):
             for a in range(A):
                 p3[t * ROWS + a * BP : t * ROWS + (a + 1) * BP, :] = control[a, 0:BP, :]
         high, low = split(p3[...])
-        wide = dot(jnp.concatenate([high, low, high], axis=1), bxd[...])
+        wide = dot(jnp.concatenate([high, high], axis=1), bxd[...]) + dot(low, bxd[0:LANES, :])
         index = lax.broadcasted_iota(jnp.int32, (256, 3 * NX), 0)
         middle = (index >= ROWS) & (index < 2 * ROWS)
         rounded = wide.astype(BF16).astype(F32)
         cs[...] = jnp.where(middle, wide - rounded, rounded).astype(BF16)
 
-    def apply(dst, j, carry):
+    def apply(j, carry):
         rows = pl.ds(pl.multiple_of(j * CHUNK, CHUNK), CHUNK)
         field = dot(kd[rows, :], cs[...])
         slopes = [g[c, rows, :].astype(F32) for c in range(3)]
         s = slopes[0] * field[:, 0:NX]
         s = s + slopes[1] * field[:, NX : 2 * NX]
         s = s + slopes[2] * field[:, 2 * NX : 3 * NX]
-        dst[rows, :] = s
-        gather_x([slopes[c] * s for c in range(3)], j)
+        gather_x([slopes[c] * s for c in range(3)], rows)
         return carry + jnp.sum((s * s).reshape(CHUNK // 8, 8, NX), axis=0)
 
     def fold(x):
@@ -321,68 +311,55 @@
     def tile_sum(x):
         return jnp.sum(jnp.sum(x, axis=0), axis=0, keepdims=True)
 
-    def reduce_start(i, stage, value):
+    def reduce_start(stage, value):
         me, count = (e, ny) if stage == 0 else (d, nz)
-        ars[i, stage] = value
-        arr[i, stage, me] = value
+        ars[stage] = value
+        arr[stage, me] = value
 
         def send(k, carry):
             other = lax.rem(me + k, count)
             z, y = (d, other) if stage == 0 else (other, e)
-            remote(ars.at[i, stage], arr.at[i, stage, me], ass.at[i, stage, k], arsem.at[i, stage, me], z, y).start()
+            remote(ars.at[stage], arr.at[stage, me], ass.at[stage, k], arsem.at[stage, me], z, y).start()
             return carry
 
         lax.fori_loop(1, count, send, 0)
 
-    def reduce_end(i, stage):
+    def reduce_end(stage):
         me, count = (e, ny) if stage == 0 else (d, nz)
 
         def take(k, carry):
             other = lax.rem(me + count - k, count)
-            remote(ars.at[i, stage], arr.at[i, stage, other], ass.at[i, stage, k], arsem.at[i, stage, other], d, e).wait_recv()
+            remote(ars.at[stage], arr.at[stage, other], ass.at[stage, k], arsem.at[stage, other], d, e).wait_recv()
             return carry
 
         lax.fori_loop(1, count, take, 0)
-        return jnp.sum(arr[i, stage], axis=0)
-
-    def scalars(i):
-        total = reduce_end(i, 1)
-        total = jnp.sum(total, axis=1, keepdims=True)
-        return total[0:1], total[1:2]
-
+        return jnp.sum(arr[stage], axis=0)
+
+    zero = jnp.zeros((8, NX), F32)
     copies0 = exchange(0)
     r0 = collect(0, copies0)
     spread_x(r0)
-    square = tile_sum(r0 * r0 * own)
-    zero = jnp.zeros((8, NX), F32)
-    energy = fold(lax.fori_loop(0, STEPS, functools.partial(apply, s0), zero))
+    energy0 = fold(lax.fori_loop(0, STEPS, apply, zero))
     copies1 = exchange(1)
-    reduce_start(0, 0, jnp.concatenate([square, energy], axis=0))
-    w0 = collect(1, copies1) + DAMPING * r0
-    reduce_start(0, 1, reduce_end(0, 0))
-    spread_x(w0)
-    lax.fori_loop(0, STEPS, functools.partial(apply, sw), zero)
+    t = collect(1, copies1)
+    spread_x(t)
+    energy1 = fold(lax.fori_loop(0, STEPS, apply, zero))
+    sums = [tile_sum(r0 * r0 * own), energy0, tile_sum(t * t * own), energy1]
+    reduce_start(0, jnp.concatenate(sums, axis=0))
     copies2 = exchange(2)
-    rr0, energy0 = scalars(0)
-    alpha0 = rr0 / (energy0 + DAMPING * rr0)
-    r1 = r0 - alpha0.reshape(1, 1, 1) * w0
-
-    def combine(j, carry):
-        rows = pl.ds(pl.multiple_of(j * CHUNK, CHUNK), CHUNK)
-        s = s0[rows, :] - alpha0 * sw[rows, :]
-        return carry + jnp.sum((s * s).reshape(CHUNK // 8, 8, NX), axis=0)
-
-    energy = fold(lax.fori_loop(0, STEPS, combine, zero))
-    reduce_start(1, 0, jnp.concatenate([tile_sum(r1 * r1 * own), energy], axis=0))
-    v = collect(2, copies2) + DAMPING * w0
-    reduce_start(1, 1, reduce_end(1, 0))
-    rr1, energy1 = scalars(1)
-    beta = rr1 / rr0
-    product = energy1 + DAMPING * rr1 - beta * rr1 / alpha0
-    alpha1 = rr1 / product
-    alpha0, alpha1, beta = (x.reshape(1, 1, 1) for x in (alpha0, alpha1, beta))
+    reduce_start(1, reduce_end(0))
+    t2 = collect(2, copies2)
+    total = jnp.sum(reduce_end(1), axis=1, keepdims=True)
+    rr0 = total[0:1]
+    m1, m2, m3 = (total[k : k + 1] / rr0 for k in (1, 2, 3))
+    alpha0 = 1.0 / (m1 + DAMPING)
+    beta = alpha0 * alpha0 * (m2 - m1 * m1)
+    curve = alpha0 * alpha0 * ((m3 - m1 * m2) - m1 * (m2 - m1 * m1)) + DAMPING * beta
+    alpha1 = beta / (curve - beta * beta / alpha0)
+    m1, alpha0, alpha1, beta = (x.reshape(1, 1, 1) for x in (m1, alpha0, alpha1, beta))
+    r1 = alpha0 * (m1 * r0 - t)
     direction = r1 + beta * r0
-    along = w0 - alpha0 * v + beta * w0
+    along = alpha0 * (m1 * t - t2) + DAMPING * r1 + beta * (t + DAMPING * r0)
     update = alpha0 * r0 + alpha1 * direction
     residual = r1 - alpha1 * along
     for c in range(3):
@@ -391,15 +368,14 @@
 
     for copy in halo + copies0 + copies1 + copies2:
         copy.wait_send()
-    for i in range(2):
-        for stage in range(2):
-            count = ny if stage == 0 else nz
-
-            def sent(k, carry):
-                remote(ars.at[i, stage], arr.at[i, stage, 0], ass.at[i, stage, k], arsem.at[i, stage, 0], d, e).wait_send()
-                return carry
-
-            lax.fori_loop(1, count, sent, 0)
+    for stage in range(2):
+        count = ny if stage == 0 else nz
+
+        def sent(k, carry):
+            remote(ars.at[stage], arr.at[stage, 0], ass.at[stage, k], arsem.at[stage, 0], d, e).wait_send()
+            return carry
+
+        lax.fori_loop(1, count, sent, 0)
 
 
 def solution(mesh):
@@ -416,18 +392,19 @@
         vmem((3, CY, NX), F32), vmem((3, CY, NX), F32),
         vmem((CZ, 4, NX), F32), vmem((CZ, 4, NX), F32),
         vmem((3, CZ * CY, NX), BF16),
-        vmem((CZ * CY, NX), F32), vmem((CZ * CY, NX), F32),
         vmem((CZ * CY, 2 * LANES), BF16),
         vmem((256, 3 * NX), BF16),
         vmem((256, LANES), F32),
+        vmem((A, B, LANES), F32),
     ] + [vmem(t.shape, BF16) for t in tables] + [
         vmem((3, A, B, LANES), F32),
+        vmem((3, 2, A, 4, LANES), F32),
         vmem((3, 2, 3, B, LANES), F32),
-        vmem((3, 2, A, 8, LANES), F32),
-        vmem((3, 4, 3, 8, LANES), F32),
-        vmem((2, 2, 2, LANES), F32),
-        vmem((2, 2, count, 2, LANES), F32),
-        dma((15,)), dma((4,)), dma((4,)), dma((3, 8)), dma((3, 8)), dma((2, 2, count)), dma((2, 2, count)),
+        vmem((3, 2, A, 4, LANES), F32),
+        vmem((3, 4, 3, 4, LANES), F32),
+        vmem((2, 4, LANES), F32),
+        vmem((2, count, 4, LANES), F32),
+        dma((15,)), dma((4,)), dma((4,)), dma((3, 8)), dma((3, 8)), dma((2, count)), dma((2, count)),
     ]
     out = jax.ShapeDtypeStruct((3, CA, CB, CE), F32)
     call = pl.pallas_call(

time: 62.5 us -> 53.4 us (0.85)
  Pallas kernels: 58.8 us -> 49.8 us
    pallas_call x1, Pallas kernels: 58.8 us -> 49.8 us  [shards(): return call(fixed, moving, *[jnp.asarray(t) for t in tables])]
where the time goes in v2:
time: 53.4 us; the launch traced here: 53.2 us
  Pallas kernels  49.8 us (93%)
  local copies, waits for them, and re-layouts  2.84 us (5%)
  between operations  0.64 us (1%)
    pallas_call x1, Pallas kernels, shards(): return call(fixed, moving, *[jnp.asarray(t) for t in tables])  49.8 us
    unnamed x2, local copies, waits for them, and re-layouts  2.84 us

profile of v2, /device:TPU:1, one launch (start us, length us, event | category | flops | bytes accessed | tf_op | source)
XLA Modules:
  0.0 53.2 jit_solution(10764566840932052447)
XLA Ops:
  0.6 49.8 %cg_step.1 = (f32[3,4,8,32]{3,2,1,0:T(8,128)}, f32[3,4,8,32]{3,2,1,0:T(8,128)}) custom-call(f32[32,64,256]{2,1,0:T(8,128)} %fixed.1, f32[32,64,256]{2,1,0:T(8,128)} %moving.1, bf16[2048,256]{1,0:T(8,128)(2,1)} %constant.10.clone.kd_h, bf16[224,2048]{1,0:T(8,128)(2,1)} %constant.11.clone.ke_h, bf16[256,768]{1,0:T(8,128)(2,1)} %constant.12.clone.bxd_h, ...), custom_call_target="tpu_custom_call" | custom-call | tf_op jit(solution)/shard_map/cg_step/pallas_call | solution.py:421
  50.4 1.4 %copy.11 = f32[3,4,8,32]{3,2,1,0:T(8,128)} copy(f32[3,4,8,32]{3,2,1,0:T(8,128)} %get-tuple-element.4) | data formatting | bytes 24576
  51.8 1.4 %copy.12 = f32[3,4,8,32]{3,2,1,0:T(8,128)} copy(f32[3,4,8,32]{3,2,1,0:T(8,128)} %get-tuple-element.5) | data formatting | bytes 24576

commit v3 on v2

--- a/solution.py
+++ b/solution.py
@@ -15,7 +15,7 @@
 A, B, LANES = 7, 16, 128
 BP = 12
 ROWS = A * BP
-CHUNK = 1024
+CHUNK = 2048
 STEPS = CZ * CY // CHUNK
 INNER = 8
 OUTER = 4
@@ -85,9 +85,9 @@
     return jnp.dot(a, b, preferred_element_type=F32)
 
 
-def kernel(nz, ny, fixed, moving, kd_h, ke_h, bxd_h, bxe_h, dx_h, upd, res,
+def kernel(nz, ny, fixed, moving, kd_h, ke_h, bxd_h, bxe_h, dx_h, out,
            fv, mv, mp, fl, ml, fh, mh, yls, yhs, zlr, zhr, ylr, yhr,
-           g, u, cs, p3, tot, kd, ke, bxd, bxe, dx,
+           g, along_s, u, cs, p3, tot, kd, ke, bxd, bxe, dx,
            enc, yst, rz, ry, rc, ars, arr,
            lsem, hss, hrs, xss, xrs, ass, arsem):
     d = lax.axis_index("gz")
@@ -95,6 +95,14 @@
     up, down = lax.rem(d + 1, nz), lax.rem(d + nz - 1, nz)
     right, left = lax.rem(e + 1, ny), lax.rem(e + ny - 1, ny)
 
+    has_down, has_up, has_left, has_right = d > 0, d < nz - 1, e > 0, e < ny - 1
+
+    def clear(missing, refs):
+        @pl.when(jnp.logical_not(missing))
+        def _():
+            for ref in refs:
+                ref[...] = jnp.zeros(ref.shape, F32)
+
     barrier = pltpu.get_barrier_semaphore()
 
     def greet_y(k, carry):
@@ -110,6 +118,15 @@
             pl.semaphore_signal(barrier, inc=1, device_id=(z, y), device_id_type=MESH)
     lax.fori_loop(1, ny, greet_y, 0)
     lax.fori_loop(1, nz, greet_z, 0)
+
+    clear(has_down, [zlr] + [rz.at[k, 0] for k in range(3)])
+    clear(has_up, [zhr] + [rz.at[k, 1] for k in range(3)])
+    clear(has_left, [ylr] + [ry.at[k, 0] for k in range(3)])
+    clear(has_right, [yhr] + [ry.at[k, 1] for k in range(3)])
+    clear(has_down & has_left, [rc.at[k, 0] for k in range(3)])
+    clear(has_down & has_right, [rc.at[k, 1] for k in range(3)])
+    clear(has_up & has_left, [rc.at[k, 2] for k in range(3)])
+    clear(has_up & has_right, [rc.at[k, 3] for k in range(3)])
 
     def local(k, src, dst):
         copy = pltpu.make_async_copy(src, dst, lsem.at[k])
@@ -144,10 +161,6 @@
         copy.wait()
     for z in (0, 1, 2, CZ - 3, CZ - 2, CZ - 1):
         mp[z + 3, 8 : 8 + CY, :] = 0.5 * (fv[z] + mv[z])
-    for copy in faces_y:
-        copy.wait()
-    yls[...] = 0.5 * (fl[:, 0:4, :] + ml[:, 0:4, :])
-    yhs[...] = 0.5 * (fh[:, 4:8, :] + mh[:, 4:8, :])
     pl.semaphore_wait(barrier, 4 + (ny - 1) + (nz - 1))
     halo = [
         remote(mp.at[pl.ds(CZ, 3), pl.ds(8, CY)], zlr, hss.at[0], hrs.at[0], up, e),
@@ -155,13 +168,14 @@
         remote(yhs, ylr, hss.at[2], hrs.at[2], d, right),
         remote(yls, yhr, hss.at[3], hrs.at[3], d, left),
     ]
-    for copy in halo:
-        copy.start()
-
-    has_down = jnp.where(d > 0, 1.0, 0.0).astype(F32)
-    has_up = jnp.where(d < nz - 1, 1.0, 0.0).astype(F32)
-    has_left = jnp.where(e > 0, 1.0, 0.0).astype(F32)
-    has_right = jnp.where(e < ny - 1, 1.0, 0.0).astype(F32)
+    pl.when(has_up)(halo[0].start)
+    pl.when(has_down)(halo[1].start)
+    for copy in faces_y:
+        copy.wait()
+    yls[...] = 0.5 * (fl[:, 0:4, :] + ml[:, 0:4, :])
+    yhs[...] = 0.5 * (fh[:, 4:8, :] + mh[:, 4:8, :])
+    pl.when(has_right)(halo[2].start)
+    pl.when(has_left)(halo[3].start)
     p3[...] = jnp.zeros_like(p3)
 
     for copy in rest:
@@ -174,10 +188,10 @@
 
     lax.fori_loop(3, CZ - 3, fill, 0)
 
-    halo[2].wait_recv()
-    mp[3 : CZ + 3, 4:8, :] = has_left * ylr[...]
-    halo[3].wait_recv()
-    mp[3 : CZ + 3, 8 + CY : 12 + CY, :] = has_right * yhr[...]
+    pl.when(has_left)(halo[2].wait_recv)
+    mp[3 : CZ + 3, 4:8, :] = ylr[...]
+    pl.when(has_right)(halo[3].wait_recv)
+    mp[3 : CZ + 3, 8 + CY : 12 + CY, :] = yhr[...]
 
     def gather_x(volume, rows):
         total = None
@@ -221,10 +235,10 @@
         return carry
 
     lax.fori_loop(0, (CZ - 2 * OUTER) // INNER, first_inner, 0)
-    halo[0].wait_recv()
-    mp[0:3, 8 : 8 + CY, :] = has_down * zlr[...]
-    halo[1].wait_recv()
-    mp[CZ + 3 : CZ + 6, 8 : 8 + CY, :] = has_up * zhr[...]
+    pl.when(has_down)(halo[0].wait_recv)
+    mp[0:3, 8 : 8 + CY, :] = zlr[...]
+    pl.when(has_up)(halo[1].wait_recv)
+    mp[CZ + 3 : CZ + 6, 8 : 8 + CY, :] = zhr[...]
 
     def first_outer(t, carry):
         first(t * (CZ - OUTER), OUTER)
@@ -236,7 +250,6 @@
 
     row = lax.broadcasted_iota(jnp.int32, (1, 4, LANES), 1)
     low_rows = jnp.where(row < 3, 1.0, 0.0).astype(F32)
-    from_right = has_right * low_rows
     pa = lax.broadcasted_iota(jnp.int32, (A, B, LANES), 0) + (d * CA - 1)
     pb = lax.broadcasted_iota(jnp.int32, (A, B, LANES), 1) + (e * CB - 1)
     ia = lax.broadcasted_iota(jnp.int32, (A, B, LANES), 0)
@@ -244,6 +257,11 @@
     inside = (pa >= 0) & (pa < nz * CA) & (pb >= 0) & (pb < ny * CB) & (ib < 11)
     inside = jnp.where(inside, 1.0, 0.0).astype(F32)
     own = jnp.where((ia >= 1) & (ia < 1 + CA) & (ib >= 1) & (ib < 1 + CB), 1.0, 0.0).astype(F32)
+
+    targets = (has_up & has_right, has_up & has_left, has_down & has_right, has_down & has_left,
+               has_up, has_down, has_right, has_left)
+    sources = (has_down & has_left, has_down & has_right, has_up & has_left, has_up & has_right,
+               has_down, has_up, has_left, has_right)
 
     def exchange(k):
         both = dot(ke[...], u[...])
@@ -265,22 +283,22 @@
             remote(after, ry.at[k, 0], xss.at[k, 6], xrs.at[k, 6], d, right),
             remote(before, ry.at[k, 1], xss.at[k, 7], xrs.at[k, 7], d, left),
         ]
-        for copy in copies:
-            copy.start()
+        for copy, target in zip(copies, targets):
+            pl.when(target)(copy.start)
         return copies
 
     def collect(k, copies):
-        for copy in copies:
-            copy.wait_recv()
+        for copy, source in zip(copies, sources):
+            pl.when(source)(copy.wait_recv)
         tot[...] = enc[k]
-        tot[0:3] += has_down * rz[k, 0]
-        tot[4:7] += has_up * rz[k, 1]
-        tot[:, 0:4] += has_left * ry[k, 0]
-        tot[:, 8:12] += from_right * ry[k, 1]
-        tot[0:3, 0:4] += (has_down * has_left) * rc[k, 0]
-        tot[0:3, 8:12] += has_down * from_right * rc[k, 1]
-        tot[4:7, 0:4] += (has_up * has_left) * rc[k, 2]
-        tot[4:7, 8:12] += has_up * from_right * rc[k, 3]
+        tot[0:3] += rz[k, 0]
+        tot[4:7] += rz[k, 1]
+        tot[:, 0:4] += ry[k, 0]
+        tot[:, 8:12] += low_rows * ry[k, 1]
+        tot[0:3, 0:4] += rc[k, 0]
+        tot[0:3, 8:12] += low_rows * rc[k, 1]
+        tot[4:7, 0:4] += rc[k, 2]
+        tot[4:7, 8:12] += low_rows * rc[k, 3]
         return tot[...] * inside
 
     def spread_x(control):
@@ -294,15 +312,34 @@
         rounded = wide.astype(BF16).astype(F32)
         cs[...] = jnp.where(middle, wide - rounded, rounded).astype(BF16)
 
-    def apply(j, carry):
-        rows = pl.ds(pl.multiple_of(j * CHUNK, CHUNK), CHUNK)
+    def through(rows):
         field = dot(kd[rows, :], cs[...])
         slopes = [g[c, rows, :].astype(F32) for c in range(3)]
         s = slopes[0] * field[:, 0:NX]
         s = s + slopes[1] * field[:, NX : 2 * NX]
         s = s + slopes[2] * field[:, 2 * NX : 3 * NX]
-        gather_x([slopes[c] * s for c in range(3)], rows)
+        return slopes, s
+
+    def add_square(carry, s):
         return carry + jnp.sum((s * s).reshape(CHUNK // 8, 8, NX), axis=0)
+
+    def step(j):
+        return pl.ds(pl.multiple_of(j * CHUNK, CHUNK), CHUNK)
+
+    def apply(j, carry):
+        slopes, s = through(step(j))
+        gather_x([slopes[c] * s for c in range(3)], step(j))
+        return add_square(carry, s)
+
+    def apply_forward(j, carry):
+        unused, s = through(step(j))
+        along_s[step(j), :] = s
+        return add_square(carry, s)
+
+    def apply_back(j, carry):
+        s = along_s[step(j), :]
+        gather_x([g[c, step(j), :].astype(F32) * s for c in range(3)], step(j))
+        return carry
 
     def fold(x):
         total = jnp.sum(x, axis=0, keepdims=True)
@@ -316,24 +353,16 @@
         ars[stage] = value
         arr[stage, me] = value
 
-        def send(k, carry):
+        for k in sorted(range(1, count), key=lambda k: -min(k, count - k)):
             other = lax.rem(me + k, count)
             z, y = (d, other) if stage == 0 else (other, e)
-            remote(ars.at[stage], arr.at[stage, me], ass.at[stage, k], arsem.at[stage, me], z, y).start()
-            return carry
-
-        lax.fori_loop(1, count, send, 0)
+            remote(ars.at[stage], arr.at[stage, me], ass.at[stage], arsem.at[stage], z, y).start()
 
     def reduce_end(stage):
-        me, count = (e, ny) if stage == 0 else (d, nz)
-
-        def take(k, carry):
-            other = lax.rem(me + count - k, count)
-            remote(ars.at[stage], arr.at[stage, other], ass.at[stage, k], arsem.at[stage, other], d, e).wait_recv()
-            return carry
-
-        lax.fori_loop(1, count, take, 0)
-        return jnp.sum(arr[stage], axis=0)
+        count = ny if stage == 0 else nz
+        others = arr.at[stage, pl.ds(0, count - 1)]
+        pltpu.make_async_copy(others, others, arsem.at[stage]).wait()
+        return jnp.sum(arr[stage, 0:count], axis=0)
 
     zero = jnp.zeros((8, NX), F32)
     copies0 = exchange(0)
@@ -343,9 +372,10 @@
     copies1 = exchange(1)
     t = collect(1, copies1)
     spread_x(t)
-    energy1 = fold(lax.fori_loop(0, STEPS, apply, zero))
+    energy1 = fold(lax.fori_loop(0, STEPS, apply_forward, zero))
     sums = [tile_sum(r0 * r0 * own), energy0, tile_sum(t * t * own), energy1]
     reduce_start(0, jnp.concatenate(sums, axis=0))
+    lax.fori_loop(0, STEPS, apply_back, 0)
     copies2 = exchange(2)
     reduce_start(1, reduce_end(0))
     t2 = collect(2, copies2)
@@ -360,22 +390,16 @@
     r1 = alpha0 * (m1 * r0 - t)
     direction = r1 + beta * r0
     along = alpha0 * (m1 * t - t2) + DAMPING * r1 + beta * (t + DAMPING * r0)
-    update = alpha0 * r0 + alpha1 * direction
-    residual = r1 - alpha1 * along
-    for c in range(3):
-        upd[c] = update[1 : 1 + CA, 1 : 1 + CB, c * CE : (c + 1) * CE]
-        res[c] = residual[1 : 1 + CA, 1 : 1 + CB, c * CE : (c + 1) * CE]
-
-    for copy in halo + copies0 + copies1 + copies2:
-        copy.wait_send()
+    parts = (alpha0 * r0, alpha1 * direction, r1, -alpha1 * along)
+    for k, part in enumerate(parts):
+        for c in range(3):
+            out[k, c] = part[1 : 1 + CA, 1 : 1 + CB, c * CE : (c + 1) * CE]
+
+    for copy, target in zip(halo + copies0 + copies1 + copies2, (has_up, has_down, has_right, has_left) + targets * 3):
+        pl.when(target)(copy.wait_send)
     for stage in range(2):
-        count = ny if stage == 0 else nz
-
-        def sent(k, carry):
-            remote(ars.at[stage], arr.at[stage, 0], ass.at[stage, k], arsem.at[stage, 0], d, e).wait_send()
-            return carry
-
-        lax.fori_loop(1, count, sent, 0)
+        others = arr.at[stage, pl.ds(0, (ny if stage == 0 else nz) - 1)]
+        pltpu.make_async_copy(others, others, ass.at[stage]).wait()
 
 
 def solution(mesh):
@@ -392,6 +416,7 @@
         vmem((3, CY, NX), F32), vmem((3, CY, NX), F32),
         vmem((CZ, 4, NX), F32), vmem((CZ, 4, NX), F32),
         vmem((3, CZ * CY, NX), BF16),
+        vmem((CZ * CY, NX), F32),
         vmem((CZ * CY, 2 * LANES), BF16),
         vmem((256, 3 * NX), BF16),
         vmem((256, LANES), F32),
@@ -404,21 +429,22 @@
         vmem((3, 4, 3, 4, LANES), F32),
         vmem((2, 4, LANES), F32),
         vmem((2, count, 4, LANES), F32),
-        dma((15,)), dma((4,)), dma((4,)), dma((3, 8)), dma((3, 8)), dma((2, count)), dma((2, count)),
+        dma((15,)), dma((4,)), dma((4,)), dma((3, 8)), dma((3, 8)), dma((2,)), dma((2,)),
     ]
-    out = jax.ShapeDtypeStruct((3, CA, CB, CE), F32)
+    out = jax.ShapeDtypeStruct((4, 3, CA, CB, CE), F32)
     call = pl.pallas_call(
         functools.partial(kernel, nz, ny),
-        out_shape=(out, out),
+        out_shape=out,
         in_specs=[pl.BlockSpec(memory_space=pl.ANY)] * 7,
-        out_specs=(pl.BlockSpec(memory_space=pltpu.VMEM), pl.BlockSpec(memory_space=pltpu.VMEM)),
+        out_specs=pl.BlockSpec(memory_space=pltpu.VMEM),
         scratch_shapes=scratch,
         compiler_params=pltpu.CompilerParams(collective_id=0, has_side_effects=True, vmem_limit_bytes=56 * 1024 * 1024),
         name="cg_step",
     )
 
     def shards(fixed, moving):
-        return call(fixed, moving, *[jnp.asarray(t) for t in tables])
+        parts = call(fixed, moving, *[jnp.asarray(t) for t in tables])
+        return parts[0] + parts[1], parts[2] + parts[3]
 
     return jax.shard_map(
         shards,

time: 53.4 us -> 46.6 us (0.87)
  Pallas kernels: 49.8 us -> 44.3 us
  local copies, waits for them, and re-layouts: 2.84 us -> 0 us
  other arithmetic: 0 us -> 1.52 us
    pallas_call x1, Pallas kernels: 49.8 us -> 44.3 us  [shards(): parts = call(fixed, moving, *[jnp.asarray(t) for t in tables])]
    unnamed x2 -> x0, local copies, waits for them, and re-layouts: 2.84 us -> none
    add x0 -> x1, other arithmetic: none -> 1.52 us  [shards(): return (parts[0] + parts[1], parts[2] + parts[3])]
where the time goes in v3:
time: 46.6 us; the launch traced here: 46.5 us
  Pallas kernels  44.3 us (95%)
  other arithmetic  1.52 us (3%)
  between operations  0.64 us (1%)
    pallas_call x1, Pallas kernels, shards(): parts = call(fixed, moving, *[jnp.asarray(t) for t in tables])  44.3 us
    add x1, other arithmetic, shards(): return (parts[0] + parts[1], parts[2] + parts[3])  1.52 us

profile of v3, /device:TPU:1, one launch (start us, length us, event | category | flops | bytes accessed | tf_op | source)
XLA Modules:
  0.0 46.5 jit_solution(5939242944450922512)
XLA Ops:
  0.6 44.3 %cg_step.1 = f32[4,3,4,8,32]{4,3,2,1,0:T(8,128)} custom-call(f32[32,64,256]{2,1,0:T(8,128)} %fixed.1, f32[32,64,256]{2,1,0:T(8,128)} %moving.1, bf16[2048,256]{1,0:T(8,128)(2,1)} %constant.10.clone.kd_h, bf16[224,2048]{1,0:T(8,128)(2,1)} %constant.11.clone.ke_h, bf16[256,768]{1,0:T(8,128)(2,1)} %constant.12.clone.bxd_h, ...), custom_call_target="tpu_custom_call" | custom-call | tf_op jit(solution)/shard_map/cg_step/pallas_call | solution.py:446
  45.0 1.5 %add_bitcast_fusion = (f32[3,4,8,32]{3,2,1,0:T(8,128)}, f32[3,4,8,32]{3,2,1,0:T(8,128)}) fusion(f32[4,3,4,8,32]{4,3,2,1,0:T(8,128)} %cg_step.1), kind=kLoop, calls=%fused_computation | loop fusion | flops 6144 | bytes 73728 | tf_op jit(solution)/shard_map/add | solution.py:447

commit v4 on v3

--- a/solution.py
+++ b/solution.py
@@ -15,10 +15,16 @@
 A, B, LANES = 7, 16, 128
 BP = 12
 ROWS = A * BP
-CHUNK = 2048
-STEPS = CZ * CY // CHUNK
+CHUNK = CZ * CY
 INNER = 8
 OUTER = 4
+STRIPS = CZ * CY // NX
+AT_BXE = NX
+AT_BXD = AT_BXE + 3 * NX
+AT_KE = AT_BXD + 6 * LANES
+AT_KD = AT_KE + 2 * A * B * STRIPS
+TABLE = AT_KD + CZ * CY
+VMEM_BYTES = 63 * 1024 * 1024
 MESH = pl.DeviceIdType.MESH
 F32, BF16 = jnp.float32, jnp.bfloat16
 
@@ -73,7 +79,9 @@
                 dx[v + step, v] = weight
             if v - step >= 0:
                 dx[v - step, v] = -weight
-    return kd, ke, bxd, bxe, dx.astype(jnp.bfloat16)
+    bxd = bxd.reshape(2 * LANES, 3, NX).transpose(1, 0, 2).reshape(6 * LANES, NX)
+    ke = ke.reshape(2 * A * B, STRIPS, NX).transpose(1, 0, 2).reshape(2 * A * B * STRIPS, NX)
+    return np.concatenate([dx.astype(jnp.bfloat16), bxe, bxd, ke, kd], axis=0)
 
 
 def split(x):
@@ -85,9 +93,9 @@
     return jnp.dot(a, b, preferred_element_type=F32)
 
 
-def kernel(nz, ny, fixed, moving, kd_h, ke_h, bxd_h, bxe_h, dx_h, out,
+def kernel(nz, ny, fixed, moving, tab_h, out,
            fv, mv, mp, fl, ml, fh, mh, yls, yhs, zlr, zhr, ylr, yhr,
-           g, along_s, u, cs, p3, tot, kd, ke, bxd, bxe, dx,
+           g, along_s, u, cs, p3, tot, up_x, tab,
            enc, yst, rz, ry, rc, ars, arr,
            lsem, hss, hrs, xss, xrs, ass, arsem):
     d = lax.axis_index("gz")
@@ -96,37 +104,6 @@
     right, left = lax.rem(e + 1, ny), lax.rem(e + ny - 1, ny)
 
     has_down, has_up, has_left, has_right = d > 0, d < nz - 1, e > 0, e < ny - 1
-
-    def clear(missing, refs):
-        @pl.when(jnp.logical_not(missing))
-        def _():
-            for ref in refs:
-                ref[...] = jnp.zeros(ref.shape, F32)
-
-    barrier = pltpu.get_barrier_semaphore()
-
-    def greet_y(k, carry):
-        pl.semaphore_signal(barrier, inc=1, device_id=(d, lax.rem(e + k, ny)), device_id_type=MESH)
-        return carry
-
-    def greet_z(k, carry):
-        pl.semaphore_signal(barrier, inc=1, device_id=(lax.rem(d + k, nz), e), device_id_type=MESH)
-        return carry
-
-    for z in (up, down):
-        for y in (right, left):
-            pl.semaphore_signal(barrier, inc=1, device_id=(z, y), device_id_type=MESH)
-    lax.fori_loop(1, ny, greet_y, 0)
-    lax.fori_loop(1, nz, greet_z, 0)
-
-    clear(has_down, [zlr] + [rz.at[k, 0] for k in range(3)])
-    clear(has_up, [zhr] + [rz.at[k, 1] for k in range(3)])
-    clear(has_left, [ylr] + [ry.at[k, 0] for k in range(3)])
-    clear(has_right, [yhr] + [ry.at[k, 1] for k in range(3)])
-    clear(has_down & has_left, [rc.at[k, 0] for k in range(3)])
-    clear(has_down & has_right, [rc.at[k, 1] for k in range(3)])
-    clear(has_up & has_left, [rc.at[k, 2] for k in range(3)])
-    clear(has_up & has_right, [rc.at[k, 3] for k in range(3)])
 
     def local(k, src, dst):
         copy = pltpu.make_async_copy(src, dst, lsem.at[k])
@@ -148,9 +125,39 @@
     rest = [
         local(8, fixed.at[pl.ds(3, CZ - 6)], fv.at[pl.ds(3, CZ - 6)]),
         local(9, moving.at[pl.ds(3, CZ - 6)], mv.at[pl.ds(3, CZ - 6)]),
-        local(10, dx_h, dx),
-        local(11, bxe_h, bxe),
+        local(10, tab_h.at[pl.ds(0, 4 * NX)], tab.at[pl.ds(0, 4 * NX)]),
     ]
+
+    barrier = pltpu.get_barrier_semaphore()
+
+    def greet_y(k, carry):
+        pl.semaphore_signal(barrier, inc=1, device_id=(d, lax.rem(e + k, ny)), device_id_type=MESH)
+        return carry
+
+    def greet_z(k, carry):
+        pl.semaphore_signal(barrier, inc=1, device_id=(lax.rem(d + k, nz), e), device_id_type=MESH)
+        return carry
+
+    for z in (up, down):
+        for y in (right, left):
+            pl.semaphore_signal(barrier, inc=1, device_id=(z, y), device_id_type=MESH)
+    lax.fori_loop(1, ny, greet_y, 0)
+    lax.fori_loop(1, nz, greet_z, 0)
+
+    def clear(missing, refs):
+        @pl.when(jnp.logical_not(missing))
+        def _():
+            for ref in refs:
+                ref[...] = jnp.zeros(ref.shape, F32)
+
+    clear(has_down, [zlr] + [rz.at[k, 0] for k in range(3)])
+    clear(has_up, [zhr] + [rz.at[k, 1] for k in range(3)])
+    clear(has_left, [ylr] + [ry.at[k, 0] for k in range(3)])
+    clear(has_right, [yhr] + [ry.at[k, 1] for k in range(3)])
+    clear(has_down & has_left, [rc.at[k, 0] for k in range(3)])
+    clear(has_down & has_right, [rc.at[k, 1] for k in range(3)])
+    clear(has_up & has_left, [rc.at[k, 2] for k in range(3)])
+    clear(has_up & has_right, [rc.at[k, 3] for k in range(3)])
 
     def remote(src, dst, send, recv, z, y):
         return pltpu.make_async_remote_copy(
@@ -180,7 +187,8 @@
 
     for copy in rest:
         copy.wait()
-    later = [local(12, ke_h, ke), local(13, bxd_h, bxd), local(14, kd_h, kd)]
+    tail = pl.ds(4 * NX, TABLE - 4 * NX)
+    later = [local(11, tab_h.at[tail], tab.at[tail])]
 
     def fill(z, carry):
         mp[z + 3, 8 : 8 + CY, :] = 0.5 * (fv[z] + mv[z])
@@ -188,63 +196,99 @@
 
     lax.fori_loop(3, CZ - 3, fill, 0)
 
+    def gather_x(volume):
+        total = None
+        for c in range(3):
+            if volume[c] is None:
+                continue
+            term = dot(volume[c].astype(BF16), tab[AT_BXE + c * NX : AT_BXE + (c + 1) * NX, :])
+            total = term if total is None else total + term
+        return total[:, :LANES] + total[:, LANES:]
+
+    def keep(total):
+        high, low = split(total)
+        u[...] = jnp.concatenate([high, low], axis=1).reshape(CZ, CY, 2 * LANES)
+
+    edges, middle, every = ((0, 16), (CY - 16, 16)), ((16, CY - 32),), ((0, CY),)
+
+    def first(z, layers, spans, parts, begun, done):
+        count = layers * sum(size for unused, size in spans)
+        deep = pl.ds(z, layers)
+
+        def block(ref, dz, dy):
+            pieces = [ref[pl.ds(z + dz, layers), dy + y : dy + y + size, :] for y, size in spans]
+            whole = pieces[0] if len(pieces) == 1 else jnp.concatenate(pieces, axis=1)
+            return whole.reshape(count, whole.shape[-1])
+
+        def put(ref, value):
+            value = value.reshape(layers, -1, value.shape[-1])
+            at = 0
+            for y, size in spans:
+                ref[deep, y : y + size, :] = value[:, at : at + size]
+                at += size
+
+        def difference(part):
+            return 45.0 * (part(1) - part(-1)) - 9.0 * (part(2) - part(-2)) + (part(3) - part(-3))
+
+        mismatch = block(fv, 0, 0) - block(mv, 0, 0)
+        volume = [None] * 3
+        for c in parts:
+            if c == 0:
+                slope = difference(lambda k: block(mp, 3 + k, 8))
+            elif c == 1:
+                slope = difference(lambda k: block(mp, 3, 8 + k))
+            else:
+                high, low = split(block(mp, 3, 8))
+                slope = dot(high, tab[0:NX, :]) + dot(low, tab[0:NX, :])
+            rounded = (slope * (1.0 / 60.0)).astype(BF16)
+            put(g.at[c], rounded)
+            volume[c] = rounded.astype(F32) * mismatch
+        total = gather_x(volume)
+        if begun:
+            total = total + block(up_x, 0, 0)
+        if not done:
+            put(up_x, total)
+        else:
+            high, low = split(total)
+            put(u, jnp.concatenate([high, low], axis=1))
+
+    inner, faces = (CZ - 2 * OUTER) // INNER, CZ - OUTER
+
+    def own_inner(t, carry):
+        first(OUTER + t * INNER, INNER, middle, (0, 1, 2), False, True)
+        first(OUTER + t * INNER, INNER, edges, (0, 2), False, False)
+        return carry
+
+    def own_outer(t, carry):
+        first(t * faces, OUTER, every, (2,), False, False)
+        return carry
+
+    def side_inner(t, carry):
+        first(OUTER + t * INNER, INNER, edges, (1,), True, True)
+        return carry
+
+    def side_outer(t, carry):
+        first(t * faces, OUTER, every, (1,), True, False)
+        return carry
+
+    def top_outer(t, carry):
+        first(t * faces, OUTER, every, (0,), True, True)
+        return carry
+
+    lax.fori_loop(0, inner, own_inner, 0)
+    lax.fori_loop(0, 2, own_outer, 0)
     pl.when(has_left)(halo[2].wait_recv)
     mp[3 : CZ + 3, 4:8, :] = ylr[...]
     pl.when(has_right)(halo[3].wait_recv)
     mp[3 : CZ + 3, 8 + CY : 12 + CY, :] = yhr[...]
 
-    def gather_x(volume, rows):
-        total = None
-        for c in range(3):
-            term = dot(volume[c].astype(BF16), bxe[c * NX : (c + 1) * NX, :])
-            total = term if total is None else total + term
-        high, low = split(total[:, :LANES] + total[:, LANES:])
-        u[rows, 0:LANES] = high
-        u[rows, LANES : 2 * LANES] = low
-
-    def first(z, layers):
-        count = layers * CY
-        rows = pl.ds(pl.multiple_of(z * CY, CY * OUTER), count)
-
-        def along_z(k):
-            return mp[pl.ds(z + 3 + k, layers), 8 : 8 + CY, :]
-
-        def along_y(k):
-            return mp[pl.ds(z + 3, layers), 8 + k : 8 + k + CY, :]
-
-        def difference(part):
-            return 45.0 * (part(1) - part(-1)) - 9.0 * (part(2) - part(-2)) + (part(3) - part(-3))
-
-        high, low = split(along_z(0).reshape(count, NX))
-        sixtieth = 1.0 / 60.0
-        slopes = (
-            difference(along_z).reshape(count, NX),
-            difference(along_y).reshape(count, NX),
-            dot(high, dx[...]) + dot(low, dx[...]),
-        )
-        mismatch = (fv[pl.ds(z, layers)] - mv[pl.ds(z, layers)]).reshape(count, NX)
-        volume = []
-        for c in range(3):
-            rounded = (slopes[c] * sixtieth).astype(BF16)
-            g[c, rows, :] = rounded
-            volume.append(rounded.astype(F32) * mismatch)
-        gather_x(volume, rows)
-
-    def first_inner(t, carry):
-        first(OUTER + t * INNER, INNER)
-        return carry
-
-    lax.fori_loop(0, (CZ - 2 * OUTER) // INNER, first_inner, 0)
+    lax.fori_loop(0, inner, side_inner, 0)
+    lax.fori_loop(0, 2, side_outer, 0)
     pl.when(has_down)(halo[0].wait_recv)
     mp[0:3, 8 : 8 + CY, :] = zlr[...]
     pl.when(has_up)(halo[1].wait_recv)
     mp[CZ + 3 : CZ + 6, 8 : 8 + CY, :] = zhr[...]
-
-    def first_outer(t, carry):
-        first(t * (CZ - OUTER), OUTER)
-        return carry
-
-    lax.fori_loop(0, 2, first_outer, 0)
+    lax.fori_loop(0, 2, top_outer, 0)
     for copy in later:
         copy.wait()
 
@@ -264,8 +308,13 @@
                has_down, has_up, has_left, has_right)
 
     def exchange(k):
-        both = dot(ke[...], u[...])
         half = A * B
+        both = None
+        for n in range(STRIPS):
+            strip = tab[AT_KE + n * 2 * half : AT_KE + (n + 1) * 2 * half, :]
+            layers = NX // CY
+            term = dot(strip, u[n * layers : (n + 1) * layers].reshape(NX, 2 * LANES))
+            both = term if both is None else both + term
         total = both[:half, :LANES] + both[half:, :LANES] + both[:half, LANES:]
         total = total.reshape(A, B, LANES)
         enc[k] = total
@@ -306,40 +355,44 @@
             for a in range(A):
                 p3[t * ROWS + a * BP : t * ROWS + (a + 1) * BP, :] = control[a, 0:BP, :]
         high, low = split(p3[...])
-        wide = dot(jnp.concatenate([high, high], axis=1), bxd[...]) + dot(low, bxd[0:LANES, :])
+        twice = jnp.concatenate([high, high], axis=1)
+        wide = []
+        for c in range(3):
+            at = AT_BXD + c * 2 * LANES
+            wide.append(dot(twice, tab[at : at + 2 * LANES, :]) + dot(low, tab[at : at + LANES, :]))
+        wide = jnp.concatenate(wide, axis=1)
         index = lax.broadcasted_iota(jnp.int32, (256, 3 * NX), 0)
         middle = (index >= ROWS) & (index < 2 * ROWS)
         rounded = wide.astype(BF16).astype(F32)
         cs[...] = jnp.where(middle, wide - rounded, rounded).astype(BF16)
 
-    def through(rows):
-        field = dot(kd[rows, :], cs[...])
-        slopes = [g[c, rows, :].astype(F32) for c in range(3)]
+    def slope(c):
+        return g[c].reshape(CHUNK, NX).astype(F32)
+
+    def through():
+        field = dot(tab[AT_KD : AT_KD + CHUNK, :], cs[...])
+        slopes = [slope(c) for c in range(3)]
         s = slopes[0] * field[:, 0:NX]
         s = s + slopes[1] * field[:, NX : 2 * NX]
         s = s + slopes[2] * field[:, 2 * NX : 3 * NX]
         return slopes, s
 
-    def add_square(carry, s):
-        return carry + jnp.sum((s * s).reshape(CHUNK // 8, 8, NX), axis=0)
-
-    def step(j):
-        return pl.ds(pl.multiple_of(j * CHUNK, CHUNK), CHUNK)
-
-    def apply(j, carry):
-        slopes, s = through(step(j))
-        gather_x([slopes[c] * s for c in range(3)], step(j))
-        return add_square(carry, s)
-
-    def apply_forward(j, carry):
-        unused, s = through(step(j))
-        along_s[step(j), :] = s
-        return add_square(carry, s)
-
-    def apply_back(j, carry):
-        s = along_s[step(j), :]
-        gather_x([g[c, step(j), :].astype(F32) * s for c in range(3)], step(j))
-        return carry
+    def square_sum(s):
+        return fold(jnp.sum((s * s).reshape(CHUNK // 8, 8, NX), axis=0))
+
+    def apply():
+        slopes, s = through()
+        keep(gather_x([slopes[c] * s for c in range(3)]))
+        return square_sum(s)
+
+    def apply_forward():
+        unused, s = through()
+        along_s[...] = s
+        return square_sum(s)
+
+    def apply_back():
+        s = along_s[...]
+        keep(gather_x([slope(c) * s for c in range(3)]))
 
     def fold(x):
         total = jnp.sum(x, axis=0, keepdims=True)
@@ -364,18 +417,17 @@
         pltpu.make_async_copy(others, others, arsem.at[stage]).wait()
         return jnp.sum(arr[stage, 0:count], axis=0)
 
-    zero = jnp.zeros((8, NX), F32)
     copies0 = exchange(0)
     r0 = collect(0, copies0)
     spread_x(r0)
-    energy0 = fold(lax.fori_loop(0, STEPS, apply, zero))
+    energy0 = apply()
     copies1 = exchange(1)
     t = collect(1, copies1)
     spread_x(t)
-    energy1 = fold(lax.fori_loop(0, STEPS, apply_forward, zero))
+    energy1 = apply_forward()
     sums = [tile_sum(r0 * r0 * own), energy0, tile_sum(t * t * own), energy1]
     reduce_start(0, jnp.concatenate(sums, axis=0))
-    lax.fori_loop(0, STEPS, apply_back, 0)
+    apply_back()
     copies2 = exchange(2)
     reduce_start(1, reduce_end(0))
     t2 = collect(2, copies2)
@@ -415,13 +467,14 @@
         vmem((CZ, 4, NX), F32), vmem((CZ, 4, NX), F32),
         vmem((3, CY, NX), F32), vmem((3, CY, NX), F32),
         vmem((CZ, 4, NX), F32), vmem((CZ, 4, NX), F32),
-        vmem((3, CZ * CY, NX), BF16),
+        vmem((3, CZ, CY, NX), BF16),
         vmem((CZ * CY, NX), F32),
-        vmem((CZ * CY, 2 * LANES), BF16),
+        vmem((CZ, CY, 2 * LANES), BF16),
         vmem((256, 3 * NX), BF16),
         vmem((256, LANES), F32),
         vmem((A, B, LANES), F32),
-    ] + [vmem(t.shape, BF16) for t in tables] + [
+        vmem((CZ, CY, LANES), F32),
+        vmem((TABLE, NX), BF16),
         vmem((3, A, B, LANES), F32),
         vmem((3, 2, A, 4, LANES), F32),
         vmem((3, 2, 3, B, LANES), F32),
@@ -429,21 +482,21 @@
         vmem((3, 4, 3, 4, LANES), F32),
         vmem((2, 4, LANES), F32),
         vmem((2, count, 4, LANES), F32),
-        dma((15,)), dma((4,)), dma((4,)), dma((3, 8)), dma((3, 8)), dma((2,)), dma((2,)),
+        dma((12,)), dma((4,)), dma((4,)), dma((3, 8)), dma((3, 8)), dma((2,)), dma((2,)),
     ]
     out = jax.ShapeDtypeStruct((4, 3, CA, CB, CE), F32)
     call = pl.pallas_call(
         functools.partial(kernel, nz, ny),
         out_shape=out,
-        in_specs=[pl.BlockSpec(memory_space=pl.ANY)] * 7,
+        in_specs=[pl.BlockSpec(memory_space=pl.ANY)] * 3,
         out_specs=pl.BlockSpec(memory_space=pltpu.VMEM),
         scratch_shapes=scratch,
-        compiler_params=pltpu.CompilerParams(collective_id=0, has_side_effects=True, vmem_limit_bytes=56 * 1024 * 1024),
+        compiler_params=pltpu.CompilerParams(collective_id=0, has_side_effects=True, vmem_limit_bytes=VMEM_BYTES),
         name="cg_step",
     )
 
     def shards(fixed, moving):
-        parts = call(fixed, moving, *[jnp.asarray(t) for t in tables])
+        parts = call(fixed, moving, jnp.asarray(tables))
         return parts[0] + parts[1], parts[2] + parts[3]
 
     return jax.shard_map(

time: 46.6 us -> 45.2 us (0.970)
  Pallas kernels: 44.3 us -> 42.9 us
    pallas_call x1, Pallas kernels: 44.3 us -> 42.9 us  [shards(): parts = call(fixed, moving, jnp.asarray(tables))]
where the time goes in v4:
time: 45.2 us; the launch traced here: 45 us
  Pallas kernels  42.9 us (95%)
  other arithmetic  1.52 us (3%)
  between operations  0.64 us (1%)
    pallas_call x1, Pallas kernels, shards(): parts = call(fixed, moving, jnp.asarray(tables))  42.9 us
    add x1, other arithmetic, shards(): return (parts[0] + parts[1], parts[2] + parts[3])  1.52 us

profile of v4, /device:TPU:1, one launch (start us, length us, event | category | flops | bytes accessed | tf_op | source)
XLA Modules:
  0.0 45.0 jit_solution(15384643663333244309)
XLA Ops:
  0.6 42.9 %cg_step.1 = f32[4,3,4,8,32]{4,3,2,1,0:T(8,128)} custom-call(f32[32,64,256]{2,1,0:T(8,128)} %fixed.1, f32[32,64,256]{2,1,0:T(8,128)} %moving.1, bf16[5632,256]{1,0:T(8,128)(2,1)} %constant.2.clone.tab_h), custom_call_target="tpu_custom_call" | custom-call | tf_op jit(solution)/shard_map/cg_step/pallas_call | solution.py:499
  43.5 1.5 %add_bitcast_fusion = (f32[3,4,8,32]{3,2,1,0:T(8,128)}, f32[3,4,8,32]{3,2,1,0:T(8,128)}) fusion(f32[4,3,4,8,32]{4,3,2,1,0:T(8,128)} %cg_step.1), kind=kLoop, calls=%fused_computation | loop fusion | flops 6144 | bytes 73728 | tf_op jit(solution)/shard_map/add | solution.py:500

commit v5 on v4

--- a/solution.py
+++ b/solution.py
@@ -13,8 +13,8 @@
 CZ, CY, NX = 32, 64, 256
 CA, CB, CE = 4, 8, 32
 A, B, LANES = 7, 16, 128
-BP = 12
-ROWS = A * BP
+BP = 11
+ROWS = 80
 CHUNK = CZ * CY
 INNER = 8
 OUTER = 4
@@ -24,7 +24,7 @@
 AT_KE = AT_BXD + 6 * LANES
 AT_KD = AT_KE + 2 * A * B * STRIPS
 TABLE = AT_KD + CZ * CY
-VMEM_BYTES = 63 * 1024 * 1024
+VMEM_BYTES = 52 * 1024 * 1024
 MESH = pl.DeviceIdType.MESH
 F32, BF16 = jnp.float32, jnp.bfloat16
 
@@ -60,8 +60,8 @@
     bz = basis_matrix(CZ, A, 1)
     by = basis_matrix(CY, B, 1)
     bx = basis_matrix(NX, CE, 0)
-    kron12 = np.einsum("za,yb->zyab", bz, by[:, :BP]).reshape(CZ * CY, ROWS)
-    high, low = halves(kron12)
+    narrow = np.einsum("za,yb->zyab", bz, by[:, :BP]).reshape(CZ * CY, A * BP)
+    high, low = halves(np.pad(narrow, ((0, 0), (0, ROWS - A * BP))))
     pad = np.zeros((CZ * CY, 256 - 3 * ROWS), jnp.bfloat16)
     kd = np.concatenate([high, high, low, pad], axis=1)
     kron16 = np.einsum("za,yb->abzy", bz, by).reshape(A * B, CZ * CY)
@@ -184,6 +184,7 @@
     pl.when(has_right)(halo[2].start)
     pl.when(has_left)(halo[3].start)
     p3[...] = jnp.zeros_like(p3)
+    cs[3 * ROWS : 256, :] = jnp.zeros((256 - 3 * ROWS, 3 * NX), BF16)
 
     for copy in rest:
         copy.wait()
@@ -351,20 +352,18 @@
         return tot[...] * inside
 
     def spread_x(control):
-        for t in range(3):
-            for a in range(A):
-                p3[t * ROWS + a * BP : t * ROWS + (a + 1) * BP, :] = control[a, 0:BP, :]
+        for a in range(A):
+            p3[a * BP : (a + 1) * BP, :] = control[a, 0:BP, :]
         high, low = split(p3[...])
         twice = jnp.concatenate([high, high], axis=1)
         wide = []
         for c in range(3):
             at = AT_BXD + c * 2 * LANES
             wide.append(dot(twice, tab[at : at + 2 * LANES, :]) + dot(low, tab[at : at + LANES, :]))
-        wide = jnp.concatenate(wide, axis=1)
-        index = lax.broadcasted_iota(jnp.int32, (256, 3 * NX), 0)
-        middle = (index >= ROWS) & (index < 2 * ROWS)
-        rounded = wide.astype(BF16).astype(F32)
-        cs[...] = jnp.where(middle, wide - rounded, rounded).astype(BF16)
+        high, low = split(jnp.concatenate(wide, axis=1))
+        cs[0:ROWS, :] = high
+        cs[ROWS : 2 * ROWS, :] = low
+        cs[2 * ROWS : 3 * ROWS, :] = high
 
     def slope(c):
         return g[c].reshape(CHUNK, NX).astype(F32)
@@ -420,12 +419,13 @@
     copies0 = exchange(0)
     r0 = collect(0, copies0)
     spread_x(r0)
+    square0 = tile_sum(r0 * r0 * own)
     energy0 = apply()
     copies1 = exchange(1)
     t = collect(1, copies1)
     spread_x(t)
-    energy1 = apply_forward()
-    sums = [tile_sum(r0 * r0 * own), energy0, tile_sum(t * t * own), energy1]
+    square1 = tile_sum(t * t * own)
+    sums = [square0, energy0, square1, apply_forward()]
     reduce_start(0, jnp.concatenate(sums, axis=0))
     apply_back()
     copies2 = exchange(2)
@@ -471,7 +471,7 @@
         vmem((CZ * CY, NX), F32),
         vmem((CZ, CY, 2 * LANES), BF16),
         vmem((256, 3 * NX), BF16),
-        vmem((256, LANES), F32),
+        vmem((ROWS, LANES), F32),
         vmem((A, B, LANES), F32),
         vmem((CZ, CY, LANES), F32),
         vmem((TABLE, NX), BF16),

time: 45.2 us -> 43.5 us (0.962)
  other arithmetic: 1.52 us -> 0.65 us
  Pallas kernels: 42.9 us -> 42.1 us
    add x1, other arithmetic: 1.52 us -> 0.65 us  [shards(): return (parts[0] + parts[1], parts[2] + parts[3])]
    pallas_call x1, Pallas kernels: 42.9 us -> 42.1 us  [shards(): parts = call(fixed, moving, jnp.asarray(tables))]
where the time goes in v5:
time: 43.5 us; the launch traced here: 43.4 us
  Pallas kernels  42.1 us (97%)
  other arithmetic  0.65 us (1%)
  between operations  0.64 us (1%)
    pallas_call x1, Pallas kernels, shards(): parts = call(fixed, moving, jnp.asarray(tables))  42.1 us

profile of v5, /device:TPU:1, one launch (start us, length us, event | category | flops | bytes accessed | tf_op | source)
XLA Modules:
  0.0 43.4 jit_solution(13961449460658624635)
XLA Ops:
  0.6 42.1 %cg_step.1 = f32[4,3,4,8,32]{4,3,2,1,0:T(8,128)S(1)} custom-call(f32[32,64,256]{2,1,0:T(8,128)} %fixed.1, f32[32,64,256]{2,1,0:T(8,128)} %moving.1, bf16[5632,256]{1,0:T(8,128)(2,1)} %constant.2.clone.tab_h), custom_call_target="tpu_custom_call" | custom-call | tf_op jit(solution)/shard_map/cg_step/pallas_call | solution.py:499
  42.8 0.6 %add_bitcast_fusion = (f32[3,4,8,32]{3,2,1,0:T(8,128)}, f32[3,4,8,32]{3,2,1,0:T(8,128)}) fusion(f32[4,3,4,8,32]{4,3,2,1,0:T(8,128)S(1)} %cg_step.1), kind=kLoop, calls=%fused_computation | loop fusion | flops 6144 | bytes 73728 | tf_op jit(solution)/shard_map/add | solution.py:500

commit v6 on v5

--- a/solution.py
+++ b/solution.py
@@ -15,7 +15,8 @@
 A, B, LANES = 7, 16, 128
 BP = 11
 ROWS = 80
-CHUNK = CZ * CY
+DEEP = 8
+CHUNK = DEEP * CY
 INNER = 8
 OUTER = 4
 STRIPS = CZ * CY // NX
@@ -130,19 +131,10 @@
 
     barrier = pltpu.get_barrier_semaphore()
 
-    def greet_y(k, carry):
-        pl.semaphore_signal(barrier, inc=1, device_id=(d, lax.rem(e + k, ny)), device_id_type=MESH)
-        return carry
-
-    def greet_z(k, carry):
-        pl.semaphore_signal(barrier, inc=1, device_id=(lax.rem(d + k, nz), e), device_id_type=MESH)
-        return carry
-
-    for z in (up, down):
-        for y in (right, left):
-            pl.semaphore_signal(barrier, inc=1, device_id=(z, y), device_id_type=MESH)
-    lax.fori_loop(1, ny, greet_y, 0)
-    lax.fori_loop(1, nz, greet_z, 0)
+    near = [(up, e), (down, e), (d, right), (d, left), (up, right), (up, left), (down, right), (down, left)]
+    far = [(d, lax.rem(e + k, ny)) for k in range(2, ny - 1)] + [(lax.rem(d + k, nz), e) for k in range(2, nz - 1)]
+    for target in near + far:
+        pl.semaphore_signal(barrier, inc=1, device_id=target, device_id_type=MESH)
 
     def clear(missing, refs):
         @pl.when(jnp.logical_not(missing))
@@ -205,10 +197,6 @@
             term = dot(volume[c].astype(BF16), tab[AT_BXE + c * NX : AT_BXE + (c + 1) * NX, :])
             total = term if total is None else total + term
         return total[:, :LANES] + total[:, LANES:]
-
-    def keep(total):
-        high, low = split(total)
-        u[...] = jnp.concatenate([high, low], axis=1).reshape(CZ, CY, 2 * LANES)
 
     edges, middle, every = ((0, 16), (CY - 16, 16)), ((16, CY - 32),), ((0, CY),)
 
@@ -365,33 +353,49 @@
         cs[ROWS : 2 * ROWS, :] = low
         cs[2 * ROWS : 3 * ROWS, :] = high
 
-    def slope(c):
-        return g[c].reshape(CHUNK, NX).astype(F32)
-
-    def through():
-        field = dot(tab[AT_KD : AT_KD + CHUNK, :], cs[...])
-        slopes = [slope(c) for c in range(3)]
-        s = slopes[0] * field[:, 0:NX]
-        s = s + slopes[1] * field[:, NX : 2 * NX]
-        s = s + slopes[2] * field[:, 2 * NX : 3 * NX]
-        return slopes, s
-
-    def square_sum(s):
-        return fold(jnp.sum((s * s).reshape(CHUNK // 8, 8, NX), axis=0))
+    def strip_of(i):
+        return slice(i * DEEP, (i + 1) * DEEP), slice(i * CHUNK, (i + 1) * CHUNK)
+
+    def decode(i):
+        unused, rows = strip_of(i)
+        weights = tab[AT_KD + i * CHUNK : AT_KD + (i + 1) * CHUNK, :]
+        return [dot(weights, cs[:, c * NX : (c + 1) * NX]) for c in range(3)]
+
+    def slopes_of(i):
+        deep, unused = strip_of(i)
+        return [g[c, deep].reshape(CHUNK, NX).astype(F32) for c in range(3)]
+
+    def along(i):
+        field, slopes = decode(i), slopes_of(i)
+        s = slopes[0] * field[0] + slopes[1] * field[1] + slopes[2] * field[2]
+        return slopes, s, jnp.sum((s * s).reshape(CHUNK // 8, 8, NX), axis=0)
+
+    def keep(i, slopes, s):
+        deep, unused = strip_of(i)
+        high, low = split(gather_x([slopes[c] * s for c in range(3)]))
+        u[deep] = jnp.concatenate([high, low], axis=1).reshape(DEEP, CY, 2 * LANES)
 
     def apply():
-        slopes, s = through()
-        keep(gather_x([slopes[c] * s for c in range(3)]))
-        return square_sum(s)
+        total = jnp.zeros((8, NX), F32)
+        for i in range(CZ // DEEP):
+            slopes, s, square = along(i)
+            keep(i, slopes, s)
+            total = total + square
+        return fold(total)
 
     def apply_forward():
-        unused, s = through()
-        along_s[...] = s
-        return square_sum(s)
+        total = jnp.zeros((8, NX), F32)
+        for i in range(CZ // DEEP):
+            unused, rows = strip_of(i)
+            unused, s, square = along(i)
+            along_s[rows, :] = s
+            total = total + square
+        return fold(total)
 
     def apply_back():
-        s = along_s[...]
-        keep(gather_x([slope(c) * s for c in range(3)]))
+        for i in range(CZ // DEEP):
+            unused, rows = strip_of(i)
+            keep(i, slopes_of(i), along_s[rows, :])
 
     def fold(x):
         total = jnp.sum(x, axis=0, keepdims=True)

time: 43.5 us -> 42.3 us (0.972)
  Pallas kernels: 42.1 us -> 40.9 us
    pallas_call x1, Pallas kernels: 42.1 us -> 40.9 us  [shards(): parts = call(fixed, moving, jnp.asarray(tables))]
where the time goes in v6:
time: 42.3 us; the launch traced here: 42.2 us
  Pallas kernels  40.9 us (97%)
  other arithmetic  0.65 us (2%)
  between operations  0.64 us (2%)
    pallas_call x1, Pallas kernels, shards(): parts = call(fixed, moving, jnp.asarray(tables))  40.9 us

profile of v6, /device:TPU:1, one launch (start us, length us, event | category | flops | bytes accessed | tf_op | source)
XLA Modules:
  0.0 42.2 jit_solution(17499160821953201271)
XLA Ops:
  0.6 40.9 %cg_step.1 = f32[4,3,4,8,32]{4,3,2,1,0:T(8,128)S(1)} custom-call(f32[32,64,256]{2,1,0:T(8,128)} %fixed.1, f32[32,64,256]{2,1,0:T(8,128)} %moving.1, bf16[5632,256]{1,0:T(8,128)(2,1)} %constant.2.clone.tab_h), custom_call_target="tpu_custom_call" | custom-call | tf_op jit(solution)/shard_map/cg_step/pallas_call | solution.py:503
  41.5 0.6 %add_bitcast_fusion = (f32[3,4,8,32]{3,2,1,0:T(8,128)}, f32[3,4,8,32]{3,2,1,0:T(8,128)}) fusion(f32[4,3,4,8,32]{4,3,2,1,0:T(8,128)S(1)} %cg_step.1), kind=kLoop, calls=%fused_computation | loop fusion | flops 6144 | bytes 73728 | tf_op jit(solution)/shard_map/add | solution.py:504

commit v7 on v6

--- a/solution.py
+++ b/solution.py
@@ -326,13 +326,15 @@
         return copies
 
     def collect(k, copies):
-        for copy, source in zip(copies, sources):
-            pl.when(source)(copy.wait_recv)
         tot[...] = enc[k]
+        for n in (7, 6, 5, 4):
+            pl.when(sources[n])(copies[n].wait_recv)
+        tot[:, 0:4] += ry[k, 0]
+        tot[:, 8:12] += low_rows * ry[k, 1]
         tot[0:3] += rz[k, 0]
         tot[4:7] += rz[k, 1]
-        tot[:, 0:4] += ry[k, 0]
-        tot[:, 8:12] += low_rows * ry[k, 1]
+        for n in range(4):
+            pl.when(sources[n])(copies[n].wait_recv)
         tot[0:3, 0:4] += rc[k, 0]
         tot[0:3, 8:12] += low_rows * rc[k, 1]
         tot[4:7, 0:4] += rc[k, 2]

time: 42.3 us -> 42.1 us (level)
  no operation moved by 1% of the time
where the time goes in v7:
time: 42.1 us; the launch traced here: 42 us
  Pallas kernels  40.7 us (97%)
  other arithmetic  0.65 us (2%)
  between operations  0.64 us (2%)
    pallas_call x1, Pallas kernels, shards(): parts = call(fixed, moving, jnp.asarray(tables))  40.7 us

profile of v7, /device:TPU:1, one launch (start us, length us, event | category | flops | bytes accessed | tf_op | source)
XLA Modules:
  0.0 42.0 jit_solution(16907456686634433584)
XLA Ops:
  0.6 40.7 %cg_step.1 = f32[4,3,4,8,32]{4,3,2,1,0:T(8,128)S(1)} custom-call(f32[32,64,256]{2,1,0:T(8,128)} %fixed.1, f32[32,64,256]{2,1,0:T(8,128)} %moving.1, bf16[5632,256]{1,0:T(8,128)(2,1)} %constant.2.clone.tab_h), custom_call_target="tpu_custom_call" | custom-call | tf_op jit(solution)/shard_map/cg_step/pallas_call | solution.py:505
  41.4 0.6 %add_bitcast_fusion = (f32[3,4,8,32]{3,2,1,0:T(8,128)}, f32[3,4,8,32]{3,2,1,0:T(8,128)}) fusion(f32[4,3,4,8,32]{4,3,2,1,0:T(8,128)S(1)} %cg_step.1), kind=kLoop, calls=%fused_computation | loop fusion | flops 6144 | bytes 73728 | tf_op jit(solution)/shard_map/add | solution.py:506

commit v8 on v7

--- a/solution.py
+++ b/solution.py
@@ -271,13 +271,16 @@
     pl.when(has_right)(halo[3].wait_recv)
     mp[3 : CZ + 3, 8 + CY : 12 + CY, :] = yhr[...]
 
-    lax.fori_loop(0, inner, side_inner, 0)
-    lax.fori_loop(0, 2, side_outer, 0)
+    for t in range(inner):
+        side_inner(t, 0)
+    for t in range(2):
+        side_outer(t, 0)
     pl.when(has_down)(halo[0].wait_recv)
     mp[0:3, 8 : 8 + CY, :] = zlr[...]
     pl.when(has_up)(halo[1].wait_recv)
     mp[CZ + 3 : CZ + 6, 8 : 8 + CY, :] = zhr[...]
-    lax.fori_loop(0, 2, top_outer, 0)
+    for t in range(2):
+        top_outer(t, 0)
     for copy in later:
         copy.wait()
 

time: 42.1 us -> 42.3 us (level)
  no operation moved by 1% of the time
where the time goes in v8:
time: 42.3 us; the launch traced here: 42.2 us
  Pallas kernels  40.9 us (97%)
  other arithmetic  0.65 us (2%)
  between operations  0.64 us (2%)
    pallas_call x1, Pallas kernels, shards(): parts = call(fixed, moving, jnp.asarray(tables))  40.9 us

profile of v8, /device:TPU:1, one launch (start us, length us, event | category | flops | bytes accessed | tf_op | source)
XLA Modules:
  0.0 42.2 jit_solution(16601619574382634138)
XLA Ops:
  0.6 40.9 %cg_step.1 = f32[4,3,4,8,32]{4,3,2,1,0:T(8,128)S(1)} custom-call(f32[32,64,256]{2,1,0:T(8,128)} %fixed.1, f32[32,64,256]{2,1,0:T(8,128)} %moving.1, bf16[5632,256]{1,0:T(8,128)(2,1)} %constant.2.clone.tab_h), custom_call_target="tpu_custom_call" | custom-call | tf_op jit(solution)/shard_map/cg_step/pallas_call | solution.py:508
  41.6 0.6 %add_bitcast_fusion = (f32[3,4,8,32]{3,2,1,0:T(8,128)}, f32[3,4,8,32]{3,2,1,0:T(8,128)}) fusion(f32[4,3,4,8,32]{4,3,2,1,0:T(8,128)S(1)} %cg_step.1), kind=kLoop, calls=%fused_computation | loop fusion | flops 6144 | bytes 73728 | tf_op jit(solution)/shard_map/add | solution.py:509
